TPU v7x, 32 devices: a whole 2x2x4 slice. The times are simulated.
32 devices in a mesh: dp: 2 (over x), pool: 4 (over z), ep: 4 (over y, core).
Axes of the slice: x: 2, y: 2, z: 4, core: 2. Of those that a mesh axis runs over, the one named last changes fastest.
Arguments:
- hidden: bfloat16 [4096, 896], P(('dp', 'pool', 'ep')), parts along dimension 0
- k_cache: bfloat16 [2, 4096, 32, 4, 128], P(None, ('dp', 'pool', 'ep')), parts along dimension 1
- v_cache: bfloat16 [2, 4096, 32, 4, 128], P(None, ('dp', 'pool', 'ep')), parts along dimension 1
- lengths: int32 [4096], P(('dp', 'pool', 'ep')), parts along dimension 0
- w_query: bfloat16 [2, 896, 2048], replicated
- w_key: bfloat16 [2, 896, 512], replicated
- w_value: bfloat16 [2, 896, 512], replicated
- w_out: bfloat16 [2, 2048, 896], replicated
- w_router: float32 [2, 896, 256], replicated
- expert_ids: int32 [2, 4096, 8], P(None, ('dp', 'pool', 'ep')), parts along dimension 1
- w_gate: bfloat16 [2, 256, 896, 256], P(None, ('pool', 'ep'))
- w_up: bfloat16 [2, 256, 896, 256], P(None, ('pool', 'ep'))
- w_down: bfloat16 [2, 256, 256, 896], P(None, ('pool', 'ep'))
Outputs:
- output: bfloat16 [4096, 896], P(('dp', 'pool', 'ep')), parts along dimension 0
There are 2 independent parts. A program takes and returns all parts, laid end to end along the dimension named above; an argument that names none is the same for every part.
All inputs are finite; a program needn't handle non-finite values.
Results may differ from a plain program's by a relative error of at most 0.02.
Values are sent between devices in bfloat16 or wider.
A program may use at most 1 GiB of HBM per device.

v0:
```python
import jax
import jax.numpy as jnp
from jax import lax
from jax.sharding import PartitionSpec as P

EPS = 1e-6
GROUP_AXES = ('pool', 'ep')
BATCH_AXES = ('dp', 'pool', 'ep')


def rms_norm(values):
    wide = values.astype(jnp.float32)
    inv_norm = lax.rsqrt(jnp.mean(wide * wide, axis=-1, keepdims=True) + EPS)
    return (wide * inv_norm).astype(jnp.bfloat16)


def attention_layer(hidden, cache_k, cache_v, lengths, q_weight, k_weight, v_weight, o_weight):
    tok_count, seq_len, kv_heads, head_dim = cache_k.shape
    per_kv = q_weight.shape[1] // (kv_heads * head_dim)
    scale = head_dim ** -0.5
    normed = rms_norm(hidden)
    query = jnp.dot(normed, q_weight, preferred_element_type=jnp.float32).astype(jnp.bfloat16).reshape(tok_count, kv_heads, per_kv, head_dim)
    key_new = jnp.dot(normed, k_weight, preferred_element_type=jnp.float32).astype(jnp.bfloat16).reshape(tok_count, kv_heads, head_dim)
    value_new = jnp.dot(normed, v_weight, preferred_element_type=jnp.float32).astype(jnp.bfloat16).reshape(tok_count, kv_heads, head_dim)
    scores = jnp.einsum('tkgd,tskd->tkgs', query, cache_k, preferred_element_type=jnp.float32) * scale
    valid_pos = jnp.arange(seq_len)[None, :] < lengths[:, None]
    scores = jnp.where(valid_pos[:, None, None, :], scores, -jnp.inf)
    score_new = jnp.einsum('tkgd,tkd->tkg', query, key_new, preferred_element_type=jnp.float32) * scale
    peak_score = jnp.maximum(jnp.max(scores, axis=-1), score_new)
    att_probs = jnp.exp(scores - peak_score[..., None])
    new_prob = jnp.exp(score_new - peak_score)
    norm_total = jnp.sum(att_probs, axis=-1) + new_prob
    att_probs = (att_probs / norm_total[..., None]).astype(jnp.bfloat16)
    new_prob = (new_prob / norm_total).astype(jnp.bfloat16).astype(jnp.float32)
    mixed = jnp.einsum('tkgs,tskd->tkgd', att_probs, cache_v, preferred_element_type=jnp.float32)
    mixed = mixed + new_prob[..., None] * value_new.astype(jnp.float32)[:, :, None, :]
    mixed = mixed.astype(jnp.bfloat16).reshape(tok_count, kv_heads * per_kv * head_dim)
    return (hidden.astype(jnp.float32) + jnp.dot(mixed, o_weight, preferred_element_type=jnp.float32)).astype(jnp.bfloat16)


def route_gates(residual, layer_ids, r_weight):
    routed = rms_norm(residual)
    logits = jnp.dot(routed.astype(jnp.float32), r_weight, preferred_element_type=jnp.float32)
    return routed, jax.nn.softmax(jnp.take_along_axis(logits, layer_ids, axis=1), axis=-1)


def window_slots(keys, groups, capacity):
    count = keys.shape[0]
    sort_order = jnp.argsort(keys, stable=True)
    sorted_keys = keys[sort_order]
    counts = jnp.bincount(keys, length=groups + 1)
    starts = jnp.cumsum(counts) - counts
    ranks = jnp.arange(count, dtype=jnp.int32) - starts[sorted_keys]
    sorted_slot = jnp.where(sorted_keys < groups, sorted_keys * capacity + ranks, groups * capacity)
    slots = jnp.zeros((count,), jnp.int32).at[sort_order].set(sorted_slot)
    item_for_slot = jnp.full((groups * capacity,), count, jnp.int32).at[slots].set(jnp.arange(count, dtype=jnp.int32), mode='drop')
    return slots, item_for_slot


def expert_windows(rows, g_weight, u_weight, d_weight):
    first = jnp.einsum('ecd,edf->ecf', rows, g_weight, preferred_element_type=jnp.float32)
    second = jnp.einsum('ecd,edf->ecf', rows, u_weight, preferred_element_type=jnp.float32)
    inner = (jax.nn.silu(first) * second).astype(jnp.bfloat16)
    return jnp.einsum('ecf,efd->ecd', inner, d_weight, preferred_element_type=jnp.float32).astype(jnp.bfloat16)


def solution(mesh):
    group_size = mesh.shape['pool'] * mesh.shape['ep']

    def device_step(hidden, k_cache, v_cache, lengths, w_query, w_key, w_value, w_out, w_router, expert_ids, w_gate, w_up, w_down):
        tok_count, width = hidden.shape
        layers = expert_ids.shape[0]
        top = expert_ids.shape[2]
        local_experts = w_gate.shape[1]
        link_cap = 2 * tok_count * top // group_size - 1
        expert_cap = group_size * ((link_cap + local_experts - 1) // local_experts)
        for layer in range(layers):
            residual = attention_layer(hidden, k_cache[layer], v_cache[layer], lengths, w_query[layer], w_key[layer], w_value[layer], w_out[layer])
            routed, gates = route_gates(residual, expert_ids[layer], w_router[layer])
            flat_ids = expert_ids[layer].reshape(-1)
            pair_slot, pair_for_slot = window_slots(flat_ids // local_experts, group_size, link_cap)
            send_rows = jnp.take(routed, pair_for_slot // top, axis=0, mode='fill', fill_value=0)
            send_local = jnp.take(flat_ids % local_experts, pair_for_slot, mode='fill', fill_value=local_experts)
            recv_rows = lax.all_to_all(send_rows, GROUP_AXES, 0, 0, tiled=True)
            recv_local = lax.all_to_all(send_local, GROUP_AXES, 0, 0, tiled=True)
            row_slot, row_for_slot = window_slots(recv_local, local_experts, expert_cap)
            expert_in = jnp.take(recv_rows, row_for_slot, axis=0, mode='fill', fill_value=0).reshape(local_experts, expert_cap, width)
            expert_out = expert_windows(expert_in, w_gate[layer], w_up[layer], w_down[layer]).reshape(local_experts * expert_cap, width)
            back_rows = jnp.take(expert_out, row_slot, axis=0, mode='fill', fill_value=0)
            returned = lax.all_to_all(back_rows, GROUP_AXES, 0, 0, tiled=True)
            pair_out = jnp.take(returned, pair_slot, axis=0).reshape(tok_count, top, width)
            combined = jnp.sum(gates[:, :, None] * pair_out.astype(jnp.float32), axis=1)
            hidden = (residual.astype(jnp.float32) + combined).astype(jnp.bfloat16)
        return hidden

    cache_spec = P(None, BATCH_AXES, None, None, None)
    expert_spec = P(None, GROUP_AXES, None, None)
    in_specs = (P(BATCH_AXES, None), cache_spec, cache_spec, P(BATCH_AXES), P(), P(), P(), P(), P(), P(None, BATCH_AXES, None), expert_spec, expert_spec, expert_spec)
    return jax.shard_map(device_step, mesh=mesh, in_specs=in_specs, out_specs=P(BATCH_AXES, None), check_vma=False)
```

profile of v0, /device:TPU:15, one launch (start us, length us, event | category | flops | bytes accessed | tf_op | source)
XLA Modules:
  0.0 686.4 jit_solution(18365889302003134654)
XLA Ops:
  39.0 8.6 %gather_fusion.12 = s32[2032]{0:T(1024)S(1)} fusion(s32[1024]{0:T(1024)S(1)} %get-tuple-element.89, s32[2048]{0:T(1024)S(1)} %pad_clamp_fusion.3), kind=kCustom, calls=%fused_computation.8.clone | custom fusion | bytes 24384 | tf_op jit(solution)/shard_map/jit(_take)/gather | solution.py:83
  92.6 8.6 %gather_fusion.6 = s32[2032]{0:T(1024)S(1)} fusion(s32[1024]{0:T(1024)S(1)} %get-tuple-element.95, s32[2048]{0:T(1024)S(1)} %pad_clamp_fusion.7), kind=kCustom, calls=%fused_computation.2.clone | custom fusion | bytes 24384 | tf_op jit(solution)/shard_map/jit(_take)/gather | solution.py:83
  134.1 9.5 %gather_fusion.5 = bf16[2032,896]{1,0:T(8,128)(2,1)} fusion(bf16[128,896]{1,0:T(8,128)(2,1)S(1)} %multiply_convert_fusion.3, s32[2048]{0:T(1024)S(1)} %pad_clamp_fusion.5), kind=kCustom, calls=%fused_computation.1.clone | custom fusion | bytes 7290816 | tf_op jit(solution)/shard_map/jit(_take)/gather | solution.py:82
  170.6 11.8 %gather_fusion.1 = s32[2032]{0:T(1024)S(1)} fusion(s32[2032]{0:T(1024)S(1)} %all_to_all.53, s32[2048]{0:T(1024)S(1)} %pad_clamp_fusion.6), kind=kCustom, calls=%fused_computation.13 | custom fusion | bytes 24384 | tf_op jit(solution)/shard_map/gather | solution.py:50
  182.4 14.7 %scatter_custom_fusion.3 = s32[17]{0:T(128)S(1)} fusion(s32[2032]{0:T(1024)S(1)} %reshape.753, s32[2032]{0:T(1024)S(1)} %ne.101, s32[]{:T(128)} %constant.162.clone.1), kind=kCustom, calls=%fused_computation.350 | custom fusion | flops 2032 | bytes 72 | tf_op jit(solution)/shard_map/scatter-add | solution.py:51
  208.9 9.9 %scatter_custom_fusion.4 = s32[2032]{0:T(1024)S(1)} fusion(s32[2032]{0:T(1024)S(1)} %compare_select_fusion.25, s32[2032]{0:T(1024)S(1)} %fusion.117, s32[]{:T(128)} %constant.162.clone.1), kind=kCustom, calls=%fused_computation.316 | custom fusion | bytes 8132 | tf_op jit(solution)/shard_map/scatter | solution.py:55
  218.9 9.9 %scatter_custom_fusion.5 = s32[2048]{0:T(1024)S(1)} fusion(s32[2032]{0:T(1024)S(1)} %compare_select_fusion.21, s32[2032]{0:T(1024)S(1)} %iota.51, s32[]{:T(128)} %constant.170.clone.1), kind=kCustom, calls=%fused_computation.312 | custom fusion | bytes 8196 | tf_op jit(solution)/shard_map/scatter | solution.py:56
  228.9 16.4 %all-to-all-done = bf16[16,127,896]{2,1,0:T(8,128)(2,1)} async-done(((bf16[16,127,896]{2,1,0:T(8,128)(2,1)}), bf16[16,127,896]{2,1,0:T(8,128)(2,1)}, u32[]{:S(2)}, u32[]{:S(2)}) %all-to-all-start) | async-done | bytes 3641376 | tf_op jit(solution)/shard_map/all_to_all | solution.py:84
  249.1 13.0 %gather_fusion.7 = bf16[2048,896]{1,0:T(8,128)(2,1)} fusion(bf16[2032,896]{1,0:T(8,128)(2,1)} %all_to_all.50, s32[2048]{0:T(1024)S(1)} %fusion.122), kind=kCustom, calls=%fused_computation.3.clone | custom fusion | bytes 7348224 | tf_op jit(solution)/shard_map/jit(_take)/gather | solution.py:87
  272.1 11.3 %fusion.36 = bf16[16,128,896]{2,1,0:T(8,128)(2,1)} fusion(bf16[2,16,256,896]{3,2,1,0:T(8,128)(2,1)} %param.37, f32[16,128,256]{2,1,0:T(8,128)} %fusion.10, bf16[16,128,896]{2,1,0:T(8,128)(2,1)} %bitcast.297, bf16[2,16,896,256]{3,2,1,0:T(8,128)(2,1)} %param.36), kind=kOutput, calls=%fused_computation.76 | convolution fusion | flops 1884028928 | bytes 24117248 | tf_op jit(solution)/shard_map/ecf,efd->ecd/dot_general | solution.py:64
  283.4 12.9 %gather_fusion.8 = bf16[2032,896]{1,0:T(8,128)(2,1)} fusion(bf16[2048,896]{1,0:T(8,128)(2,1)} %bitcast.294, s32[2048]{0:T(1024)S(1)} %pad_clamp_fusion.4), kind=kCustom, calls=%fused_computation.4.clone | custom fusion | bytes 7290816 | tf_op jit(solution)/shard_map/jit(_take)/gather | solution.py:89
  309.7 8.6 %gather_fusion.4 = f32[1024]{0:T(1024)S(1)} fusion(f32[128,256]{1,0:T(8,128)S(1)} %fusion.84, s32[1024]{0:T(1024)S(1)} %reshape.1046), kind=kCustom, calls=%fused_computation.clone | custom fusion | bytes 16384 | tf_op jit(solution)/shard_map/jit(take_along_axis)/gather | solution.py:44
  318.8 71.7 %all-to-all-done.2 = bf16[16,127,896]{2,1,0:T(8,128)(2,1)} async-done(((bf16[16,127,896]{2,1,0:T(8,128)(2,1)}), bf16[16,127,896]{2,1,0:T(8,128)(2,1)}, u32[]{:S(2)}, u32[]{:S(2)}) %all-to-all-start.2) | async-done | bytes 3641376 | tf_op jit(solution)/shard_map/all_to_all | solution.py:90
  423.3 9.5 %gather_fusion.11 = bf16[2032,896]{1,0:T(8,128)(2,1)} fusion(bf16[128,896]{1,0:T(8,128)(2,1)S(1)} %multiply_convert_fusion.2, s32[2048]{0:T(1024)S(1)} %pad_clamp_fusion.1), kind=kCustom, calls=%fused_computation.7.clone | custom fusion | bytes 7290816 | tf_op jit(solution)/shard_map/jit(_take)/gather | solution.py:82
  445.6 14.7 %scatter_custom_fusion.9 = s32[17]{0:T(128)S(1)} fusion(s32[2032]{0:T(1024)S(1)} %reshape.801, s32[2032]{0:T(1024)S(1)} %ne.101, s32[]{:T(128)} %constant.162.clone.1), kind=kCustom, calls=%fused_computation.346 | custom fusion | flops 2032 | bytes 72 | tf_op jit(solution)/shard_map/scatter-add | solution.py:51
  465.5 11.8 %gather_fusion.3 = s32[2032]{0:T(1024)S(1)} fusion(s32[2032]{0:T(1024)S(1)} %all_to_all.62, s32[2048]{0:T(1024)S(1)} %pad_clamp_fusion.2), kind=kCustom, calls=%fused_computation.15 | custom fusion | bytes 24384 | tf_op jit(solution)/shard_map/gather | solution.py:50
  489.2 9.9 %scatter_custom_fusion.10 = s32[2032]{0:T(1024)S(1)} fusion(s32[2032]{0:T(1024)S(1)} %compare_select_fusion.24, s32[2032]{0:T(1024)S(1)} %fusion.115, s32[]{:T(128)} %constant.162.clone.1), kind=kCustom, calls=%fused_computation.314 | custom fusion | bytes 8132 | tf_op jit(solution)/shard_map/scatter | solution.py:55
  499.2 9.9 %scatter_custom_fusion.11 = s32[2048]{0:T(1024)S(1)} fusion(s32[2032]{0:T(1024)S(1)} %compare_select_fusion.18, s32[2032]{0:T(1024)S(1)} %iota.57, s32[]{:T(128)} %constant.170.clone.1), kind=kCustom, calls=%fused_computation.310 | custom fusion | bytes 8196 | tf_op jit(solution)/shard_map/scatter | solution.py:56
  509.2 17.7 %all-to-all-done.3 = bf16[16,127,896]{2,1,0:T(8,128)(2,1)} async-done(((bf16[16,127,896]{2,1,0:T(8,128)(2,1)}), bf16[16,127,896]{2,1,0:T(8,128)(2,1)}, u32[]{:S(2)}, u32[]{:S(2)}) %all-to-all-start.3) | async-done | bytes 3641376 | tf_op jit(solution)/shard_map/all_to_all | solution.py:84
  531.0 13.0 %gather_fusion.13 = bf16[2048,896]{1,0:T(8,128)(2,1)} fusion(bf16[2032,896]{1,0:T(8,128)(2,1)} %all_to_all.59, s32[2048]{0:T(1024)S(1)} %fusion.123), kind=kCustom, calls=%fused_computation.9.clone | custom fusion | bytes 7348224 | tf_op jit(solution)/shard_map/jit(_take)/gather | solution.py:87
  554.1 11.3 %fusion.39 = bf16[16,128,896]{2,1,0:T(8,128)(2,1)} fusion(bf16[2,16,256,896]{3,2,1,0:T(8,128)(2,1)} %param.37, f32[16,128,256]{2,1,0:T(8,128)} %fusion.4, bf16[16,128,896]{2,1,0:T(8,128)(2,1)} %bitcast.299, bf16[2,16,896,256]{3,2,1,0:T(8,128)(2,1)} %param.36), kind=kOutput, calls=%fused_computation.77 | convolution fusion | flops 1884028928 | bytes 24117248 | tf_op jit(solution)/shard_map/ecf,efd->ecd/dot_general | solution.py:64
  565.3 13.0 %gather_fusion.14 = bf16[2032,896]{1,0:T(8,128)(2,1)} fusion(bf16[2048,896]{1,0:T(8,128)(2,1)} %bitcast.295, s32[2048]{0:T(1024)S(1)} %pad_clamp_fusion), kind=kCustom, calls=%fused_computation.10.clone | custom fusion | bytes 7290816 | tf_op jit(solution)/shard_map/jit(_take)/gather | solution.py:89
  591.9 8.6 %gather_fusion.10 = f32[1024]{0:T(1024)S(1)} fusion(f32[128,256]{1,0:T(8,128)S(1)} %fusion.80, s32[1024]{0:T(1024)S(1)} %reshape.1061), kind=kCustom, calls=%fused_computation.6.clone | custom fusion | bytes 16384 | tf_op jit(solution)/shard_map/jit(take_along_axis)/gather | solution.py:44
  601.0 71.7 %all-to-all-done.5 = bf16[16,127,896]{2,1,0:T(8,128)(2,1)} async-done(((bf16[16,127,896]{2,1,0:T(8,128)(2,1)}), bf16[16,127,896]{2,1,0:T(8,128)(2,1)}, u32[]{:S(2)}, u32[]{:S(2)}) %all-to-all-start.5) | async-done | bytes 3641376 | tf_op jit(solution)/shard_map/all_to_all | solution.py:90
  (223 shorter events, 286.9 us)
Async XLA Ops:
  0.8 0.6 copy-start.2
  34.0 13.5 %copy-start.7 = (s32[1024]{0:T(1024)}, s32[1024]{0:T(1024)S(1)}, u32[]{:S(2)}) copy-start(s32[1024]{0:T(1024)S(1)} %scatter_custom_fusion.7) | copy-start | bytes 12292
  47.6 44.7 %copy-start.6 = (bf16[128,896]{1,0:T(8,128)(2,1)S(1)}, bf16[128,896]{1,0:T(8,128)(2,1)}, u32[]{:S(2)}) copy-start(bf16[128,896]{1,0:T(8,128)(2,1)} %param.25) | copy-start | bytes 688132
  47.6 44.9 %copy-start.10 = (s32[128]{0:T(128)S(1)}, s32[128]{0:T(128)}, u32[]{:S(2)}) copy-start(s32[128]{0:T(128)} %param.28) | copy-start | bytes 1540
  48.3 95.3 %all-to-all-start.4 = ((s32[16,127,1]{1,2,0:T(1,128)}), s32[16,127,1]{1,2,0:T(1,128)S(1)}, u32[]{:S(2)}, u32[]{:S(2)}) async-start(s32[16,127,1]{1,2,0:T(1,128)} %bitcast.89), calls=%async_computation.4 | async-start | bytes 16384 | tf_op jit(solution)/shard_map/all_to_all | solution.py:85
  92.6 8.6 %copy-start.11 = (bf16[2,896,512]{2,1,0:T(8,128)(2,1)S(1)}, bf16[2,896,512]{2,1,0:T(8,128)(2,1)}, u32[]{:S(2)}) copy-start(bf16[2,896,512]{2,1,0:T(8,128)(2,1)} %param.30) | copy-start | bytes 5505028
  143.6 13.8 %all-to-all-start.1 = ((s32[16,127,1]{1,2,0:T(1,128)}), s32[16,127,1]{1,2,0:T(1,128)S(1)}, u32[]{:S(2)}, u32[]{:S(2)}) async-start(s32[16,127,1]{1,2,0:T(1,128)} %bitcast.31), calls=%async_computation.1 | async-start | bytes 16384 | tf_op jit(solution)/shard_map/all_to_all | solution.py:85
  157.4 87.9 %all-to-all-start = ((bf16[16,127,896]{2,1,0:T(8,128)(2,1)}), bf16[16,127,896]{2,1,0:T(8,128)(2,1)}, u32[]{:S(2)}, u32[]{:S(2)}) async-start(bf16[16,127,896]{2,1,0:T(8,128)(2,1)} %all_to_all.48), calls=%async_computation | async-start | bytes 7340032 | tf_op jit(solution)/shard_map/all_to_all | solution.py:84
  264.5 1.8 copy-start
  304.0 5.4 copy-start.4
  304.0 86.5 %all-to-all-start.2 = ((bf16[16,127,896]{2,1,0:T(8,128)(2,1)}), bf16[16,127,896]{2,1,0:T(8,128)(2,1)}, u32[]{:S(2)}, u32[]{:S(2)}) async-start(bf16[16,127,896]{2,1,0:T(8,128)(2,1)} %all_to_all.54), calls=%async_computation.2 | async-start | bytes 7340032 | tf_op jit(solution)/shard_map/all_to_all | solution.py:90
  401.6 3.0 copy-start.12
  440.7 86.2 %all-to-all-start.3 = ((bf16[16,127,896]{2,1,0:T(8,128)(2,1)}), bf16[16,127,896]{2,1,0:T(8,128)(2,1)}, u32[]{:S(2)}, u32[]{:S(2)}) async-start(bf16[16,127,896]{2,1,0:T(8,128)(2,1)} %all_to_all.57), calls=%async_computation.3 | async-start | bytes 7340032 | tf_op jit(solution)/shard_map/all_to_all | solution.py:84
  546.3 1.8 copy-start.1
  586.1 5.4 copy-start.3
  586.1 5.5 copy-start.8
  586.1 5.6 copy-start.5
  586.1 86.7 %all-to-all-start.5 = ((bf16[16,127,896]{2,1,0:T(8,128)(2,1)}), bf16[16,127,896]{2,1,0:T(8,128)(2,1)}, u32[]{:S(2)}, u32[]{:S(2)}) async-start(bf16[16,127,896]{2,1,0:T(8,128)(2,1)} %all_to_all.63), calls=%async_computation.5 | async-start | bytes 7340032 | tf_op jit(solution)/shard_map/all_to_all | solution.py:90
  601.0 75.6 %copy-start.9 = (s32[1024]{0:T(1024)S(1)}, s32[1024]{0:T(1024)}, u32[]{:S(2)}) copy-start(s32[1024]{0:T(1024)} %get-tuple-element.87) | copy-start | bytes 12292
where the time goes:
time: 695 us; the launch traced here: 686 us
  local copies, waits for them, and re-layouts  271 us (39%)
  waiting for transfers between devices  178 us (26%)
  other arithmetic  137 us (20%)
  matrix products  64.2 us (9%)
  starting transfers between devices  34.6 us (5%)
    all_to_all x2, waiting for transfers between devices, device_step(): returned = lax.all_to_all(back_rows, GROUP_AXES, 0, 0, tiled=True)  143 us
    scatter-add x4, other arithmetic, window_slots(): counts = jnp.bincount(keys, length=groups + 1)  44.5 us
    all_to_all x2, waiting for transfers between devices, device_step(): recv_rows = lax.all_to_all(send_rows, GROUP_AXES, 0, 0, tiled=True)  34.1 us
    gather x4, local copies, waits for them, and re-layouts, window_slots(): sorted_keys = keys[sort_order]  32.6 us
    scatter x4, local copies, waits for them, and re-layouts, window_slots(): jnp.full((groups * capacity,), count, jnp.int32).at[slots]  28.7 us
    scatter x4, local copies, waits for them, and re-layouts, window_slots(): slots = jnp.zeros((count,), jnp.int32).at[sort_order].set(sorted_slot)  28.5 us
    gather x2, local copies, waits for them, and re-layouts, device_step(): jnp.take(recv_rows, row_for_slot, axis=0, mode='fill', fill_value=0)  25.9 us
    gather x2, local copies, waits for them, and re-layouts, device_step(): jnp.take(expert_out, row_slot, axis=0, mode='fill', fill_value=0)  25.9 us
  transfers between devices with their start and end apart: 6, of which 4 were waited for; matrix products, arithmetic and copies ran while one was open for 35% of the time, Pallas kernels for 0%

commit v1 on v0

v1 whole, which is shorter than its diff:
```python
import functools

import jax
import jax.numpy as jnp
from jax import lax
from jax.experimental import pallas as pl
from jax.experimental.pallas import tpu as pltpu
from jax.sharding import PartitionSpec as P

EPS = 1e-6
GROUP_AXES = ('pool', 'ep')
BATCH_AXES = ('dp', 'pool', 'ep')
MESH = pl.DeviceIdType.MESH
F32 = jnp.float32
BF16 = jnp.bfloat16
VMEM_LIMIT = 66_000_000

NZ, NY = 4, 2
GROUP = 16
TOK = 128
HALF = TOK // 2
D = 896
HEADS, KV, HD, SEQ = 16, 4, 128, 32
PER_KV = HEADS // KV
TOP = 8
EXPERTS, LOCAL, FF = 256, 16, 256
SLOTS = LOCAL * TOK
BLK = 16


def rms(wide):
    return wide * lax.rsqrt(jnp.mean(wide * wide, axis=-1, keepdims=True) + EPS)


def dot(a, b):
    return jnp.dot(a, b, preferred_element_type=F32)


def split3(wide):
    high = wide.astype(BF16)
    rest = wide - high.astype(F32)
    mid = rest.astype(BF16)
    low = (rest - mid.astype(F32)).astype(BF16)
    return high, mid, low


def attention_kernel(layer, x_ref, kc_hbm, vc_hbm, len_ref, wq_hbm, wk_hbm, wv_hbm, wo_hbm, wr_hbm, ids_ref,
                     a_ref, u_ref, gate_ref,
                     wq, wk, wv, wo, wr, kc, vc, qs, ks, vs, os, mixed, wsem, ksem, vsem):
    parts = 4
    step = TOK // parts
    loads = [pltpu.make_async_copy(src.at[layer], dst, wsem.at[i]) for i, (src, dst) in enumerate(
        ((wq_hbm, wq), (wk_hbm, wk), (wv_hbm, wv), (wo_hbm, wo), (wr_hbm, wr)))]
    k_loads = [pltpu.make_async_copy(kc_hbm.at[layer, pl.ds(i * step, step)], kc.at[pl.ds(i * step, step)], ksem.at[i]) for i in range(parts)]
    v_loads = [pltpu.make_async_copy(vc_hbm.at[layer, pl.ds(i * step, step)], vc.at[pl.ds(i * step, step)], vsem.at[i]) for i in range(parts)]
    for copy in loads[:3]:
        copy.start()
    for i in range(parts):
        k_loads[i].start()
        v_loads[i].start()
    for copy in loads[3:]:
        copy.start()

    x = x_ref[...].astype(F32)
    h = rms(x).astype(BF16)
    loads[0].wait()
    for c in range(4):
        q = dot(h, wq[:, c * 512:(c + 1) * 512]).astype(BF16).astype(F32)
        for j in range(4):
            qs[pl.ds(c * 4 + j, TOK, stride=HEADS), :] = q[:, j * HD:(j + 1) * HD]
    loads[1].wait()
    k_new = dot(h, wk[...]).astype(BF16).astype(F32)
    loads[2].wait()
    v_new = dot(h, wv[...]).astype(BF16).astype(F32)
    for i in range(HEADS):
        j = i // PER_KV
        ks[pl.ds(i, TOK, stride=HEADS), :] = k_new[:, j * HD:(j + 1) * HD]
        vs[pl.ds(i, TOK, stride=HEADS), :] = v_new[:, j * HD:(j + 1) * HD]

    scale = HD ** -0.5
    lane = lax.broadcasted_iota(jnp.int32, (HEADS, SEQ * KV), 1)
    head = lax.broadcasted_iota(jnp.int32, (HEADS, SEQ * KV), 0)
    own_kv = lax.rem(lane, KV) == head // PER_KV
    pos = jnp.where(own_kv, lane // KV, SEQ)

    def attend(b, carry):
        tok = b * BLK
        rows = pl.ds(tok * HEADS, BLK * HEADS)
        q_wide = qs[rows, :]
        q_blk = q_wide.astype(BF16)
        score_list, mask_list = [], []
        for t in range(BLK):
            score_list.append(lax.dot_general(q_blk[t * HEADS:(t + 1) * HEADS], kc[tok + t], (((1,), (1,)), ((), ())), preferred_element_type=F32))
            mask_list.append(pos < len_ref[0, tok + t])
        score = jnp.concatenate(score_list, axis=0) * scale
        mask = jnp.concatenate(mask_list, axis=0)
        score = jnp.where(mask, score, -jnp.inf)
        score_new = jnp.sum(q_wide * ks[rows, :], axis=-1, keepdims=True) * scale
        peak = jnp.maximum(jnp.max(score, axis=-1, keepdims=True), score_new)
        prob = jnp.exp(score - peak)
        prob_new = jnp.exp(score_new - peak)
        total = jnp.sum(prob, axis=-1, keepdims=True) + prob_new
        prob = (prob / total).astype(BF16)
        prob_new = (prob_new / total).astype(BF16).astype(F32)
        out = [dot(prob[t * HEADS:(t + 1) * HEADS], vc[tok + t]) for t in range(BLK)]
        out = jnp.concatenate(out, axis=0) + prob_new * vs[rows, :]
        os[rows, :] = out.astype(BF16).astype(F32)
        return carry

    per_part = step // BLK
    for i in range(parts):
        k_loads[i].wait()
        v_loads[i].wait()
        lax.fori_loop(i * per_part, (i + 1) * per_part, attend, 0)

    for i in range(HEADS):
        mixed[:, i * HD:(i + 1) * HD] = os[pl.ds(i, TOK, stride=HEADS), :].astype(BF16)
    loads[3].wait()
    a = (x + dot(mixed[...], wo[...])).astype(BF16)
    a_ref[...] = a
    u = rms(a.astype(F32)).astype(BF16)
    u_ref[...] = u
    loads[4].wait()
    high, mid, low = split3(wr[...])
    logits = (dot(u, low) + dot(u, mid)) + dot(u, high)
    logits = logits.T
    expert = lax.broadcasted_iota(jnp.int32, (EXPERTS, TOK), 0)
    chosen = [jnp.sum(jnp.where(expert == ids_ref[layer, k:k + 1, :], logits, 0.0), axis=0, keepdims=True) for k in range(TOP)]
    chosen = jnp.concatenate(chosen, axis=0)
    weight = jnp.exp(chosen - jnp.max(chosen, axis=0, keepdims=True))
    gate_ref[...] = weight / jnp.sum(weight, axis=0, keepdims=True)


def attention(layer, hidden, kc, vc, lengths, wq, wk, wv, wo, wr, ids):
    vmem = pl.BlockSpec(memory_space=pltpu.VMEM)
    hbm = pl.BlockSpec(memory_space=pl.ANY)
    return pl.pallas_call(
        functools.partial(attention_kernel, layer),
        out_shape=(jax.ShapeDtypeStruct((TOK, D), BF16), jax.ShapeDtypeStruct((TOK, D), BF16), jax.ShapeDtypeStruct((TOP, TOK), F32)),
        in_specs=[vmem, hbm, hbm, pl.BlockSpec(memory_space=pltpu.SMEM), hbm, hbm, hbm, hbm, hbm, vmem],
        out_specs=(vmem, vmem, vmem),
        scratch_shapes=[
            pltpu.VMEM((D, HEADS * HD), BF16), pltpu.VMEM((D, KV * HD), BF16), pltpu.VMEM((D, KV * HD), BF16),
            pltpu.VMEM((HEADS * HD, D), BF16), pltpu.VMEM((D, EXPERTS), F32),
            pltpu.VMEM((TOK, SEQ * KV, HD), BF16), pltpu.VMEM((TOK, SEQ * KV, HD), BF16),
            pltpu.VMEM((TOK * HEADS, HD), F32), pltpu.VMEM((TOK * HEADS, HD), F32), pltpu.VMEM((TOK * HEADS, HD), F32),
            pltpu.VMEM((TOK * HEADS, HD), F32), pltpu.VMEM((TOK, HEADS * HD), BF16),
            pltpu.SemaphoreType.DMA((5,)), pltpu.SemaphoreType.DMA((4,)), pltpu.SemaphoreType.DMA((4,)),
        ],
        compiler_params=pltpu.CompilerParams(vmem_limit_bytes=VMEM_LIMIT),
        name='attention',
    )(hidden, kc, vc, lengths, wq, wk, wv, wo, wr, ids)


def remote(src, dst, send, recv, target):
    return pltpu.make_async_remote_copy(src_ref=src, dst_ref=dst, send_sem=send, recv_sem=recv, device_id=target, device_id_type=MESH)


def moe_kernel(layer, u_ref, gate_ref, ids_ref, a_ref, wg_hbm, wu_hbm, wd_hbm, out_ref,
               wg, wu, wd, rows, gates, pos, jpos, tgt, xs, ys, pick,
               own_part, far_part, core_in, y_in, right_in, left_in,
               wsem, gsem_s, gsem_r, az_s, az_r, ay_s, ay_r, ac_s, ac_r,
               rc_s, rc_r, ry_s, ry_r, rr_s, rr_r, rl_s, rl_r):
    z = lax.axis_index('pool')
    ep = lax.axis_index('ep')
    y = ep // 2
    core = lax.rem(ep, 2)

    def at(zz, dy, dc):
        return {'pool': zz, 'ep': lax.rem(y + dy, 2) * 2 + lax.rem(core + dc, 2)}

    def slot(zz, dy, dc):
        return (zz * 2 + dy) * 2 + dc

    barrier = pltpu.get_barrier_semaphore()
    others = [(dz, dy, dc) for dz in range(NZ) for dy in range(NY) for dc in range(2) if (dz, dy, dc) != (0, 0, 0)]
    for dz, dy, dc in others:
        pl.semaphore_signal(barrier, inc=1, device_id=at(lax.rem(z + dz, NZ), dy, dc), device_id_type=MESH)

    chunk = 4
    weights = []
    for i in range(LOCAL // chunk):
        part = pl.ds(i * chunk, chunk)
        for j, (src, dst) in enumerate(((wg_hbm, wg), (wu_hbm, wu), (wd_hbm, wd))):
            weights.append(pltpu.make_async_copy(src.at[layer, part], dst.at[part], wsem.at[j, i]))
    for copy in weights:
        copy.start()

    pl.semaphore_wait(barrier, len(others))

    def block(zz, dy, dc, half):
        return rows.at[zz * 2 + dy, pl.ds(dc * TOK + half * HALF, HALF)]

    def own(half):
        return u_ref.at[pl.ds(half * HALF, HALF)]

    def to_z(zz, half, step):
        src = block(zz, 0, 0, half)
        return remote(src, src, az_s.at[zz, half, (step + 1) // 2], az_r.at[zz, half], at(z + step, 0, 0))

    def own_to_z(half, step):
        return remote(own(half), block(z, 0, 0, half), az_s.at[z, half, (step + 1) // 2], az_r.at[z, half], at(z + step, 0, 0))

    def to_y(zz, half):
        return remote(block(zz, 0, 0, half), block(zz, 1, 0, half), ay_s.at[zz, half], ay_r.at[zz, half], at(z, 1, 0))

    def own_to_y(half):
        return remote(own(half), block(z, 1, 0, half), ay_s.at[z, half], ay_r.at[z, half], at(z, 1, 0))

    def whole(zz, dy, dc):
        return rows.at[zz * 2 + dy, pl.ds(dc * TOK, TOK)]

    def to_core(zz, dy):
        return remote(whole(zz, dy, 0), whole(zz, dy, 1), ac_s.at[zz, dy], ac_r.at[zz, dy], at(z, 0, 1))

    def own_to_core():
        return remote(u_ref, whole(z, 0, 1), ac_s.at[z, 0], ac_r.at[z, 0], at(z, 0, 1))

    own_to_core().start()
    for half in range(2):
        @pl.when(z < NZ - 1)
        def _():
            own_to_z(half, 1).start()

        @pl.when(z > 0)
        def _():
            own_to_z(half, -1).start()
        own_to_y(half).start()

    def gate_copy(dz, dy, dc):
        me = slot(z, dy, dc)
        return remote(gate_ref, gates.at[me], gsem_s.at[dz * 4 + dy * 2 + dc], gsem_r.at[me], at(lax.rem(z + dz, NZ), dy, dc))

    for o in others:
        gate_copy(*o).start()
    gates[slot(z, 0, 0)] = gate_ref[...]
    rows[z * 2, pl.ds(0, TOK), :] = u_ref[...]

    first = (z * 4 + ep) * LOCAL
    expert = lax.broadcasted_iota(jnp.int32, (LOCAL, TOK), 0) + first
    tri = (lax.broadcasted_iota(jnp.int32, (TOK, TOK), 0) < lax.broadcasted_iota(jnp.int32, (TOK, TOK), 1)).astype(BF16)
    ones = jnp.ones((TOK, TOK), BF16)
    low = (lax.broadcasted_iota(jnp.int32, (LOCAL, LOCAL), 1) < lax.broadcasted_iota(jnp.int32, (LOCAL, LOCAL), 0)).astype(BF16)
    lane = lax.broadcasted_iota(jnp.int32, (LOCAL, TOK), 1).astype(F32)

    def source(s):
        zz = s // 4
        dy = lax.rem(s // 2, 2)
        dc = lax.rem(s, 2)
        return zz * 4 + lax.rem(y + dy, 2) * 2 + lax.rem(core + dc, 2)

    def plan(s, base):
        ids = ids_ref[source(s)]
        hit = jnp.zeros((LOCAL, TOK), F32)
        for k in range(TOP):
            hit = hit + jnp.where(expert == ids[k:k + 1, :], 1.0, 0.0)
        hit16 = hit.astype(BF16)
        rank = dot(hit16, tri)
        count = dot(hit16, ones)
        offset = dot(low, count.astype(BF16))
        pos[s] = jnp.where(hit > 0, base + rank, -1.0)
        jpos[s] = jnp.where(hit > 0, offset + rank, -1.0)
        local = lane - base
        tgt[s] = jnp.where((local >= 0) & (local < count), local + offset, -1.0)
        return base + count

    lax.fori_loop(0, GROUP, plan, jnp.zeros((LOCAL, TOK), F32))

    sub = lax.broadcasted_iota(jnp.int32, (TOK, TOK), 0).astype(F32)

    def fill(zz, dy, fresh):
        chip = zz * 2 + dy

        def body(e2, carry):
            picks = []
            for j in range(2):
                e = e2 * 2 + j
                picks.append(jnp.concatenate([(sub == pos[chip * 2 + dc, pl.ds(e, 1), :]).astype(F32).astype(BF16) for dc in range(2)], axis=1))
            got = dot(jnp.concatenate(picks, axis=0), rows[chip])
            where = pl.ds(pl.multiple_of(e2 * 2 * TOK, 2 * TOK), 2 * TOK)
            if fresh:
                xs[where, :] = got
            else:
                xs[where, :] += got
            return carry
        lax.fori_loop(0, LOCAL // 2, body, 0)

    def arrive(zz, step):
        last = (z == NZ - 1) if step == 1 else (z == 0)
        for half in range(2):
            remote(block(zz, 0, 0, half), block(zz, 0, 0, half), az_s.at[zz, half, 0], az_r.at[zz, half], at(z, 0, 1)).wait_recv()

            @pl.when(jnp.logical_not(last))
            def _():
                to_z(zz, half, step).start()
            to_y(zz, half).start()
        to_core(zz, 0).start()

    def core_recv(zz, dy):
        to_core(zz, dy).wait_recv()

    def y_recv(zz):
        for half in range(2):
            to_y(zz, half).wait_recv()
        to_core(zz, 1).start()

    core_recv(z, 0)
    fill(z, 0, True)

    for k in range(1, NZ):
        @pl.when(z - k >= 0)
        def _():
            arrive(z - k, 1)

        @pl.when(z + k < NZ)
        def _():
            arrive(z + k, -1)
        if k == 1:
            y_recv(z)

        @pl.when(z - k >= 0)
        def _():
            core_recv(z - k, 0)
            fill(z - k, 0, False)

        @pl.when(z + k < NZ)
        def _():
            core_recv(z + k, 0)
            fill(z + k, 0, False)
        if k == 1:
            core_recv(z, 1)
            fill(z, 1, False)
    for k in range(1, NZ):
        zz = lax.rem(z + k, NZ)
        y_recv(zz)
        core_recv(zz, 1)
        fill(zz, 1, False)

    def experts(e, carry):
        window = pl.ds(pl.multiple_of(e * TOK, TOK), TOK)
        x = xs[window, :].astype(BF16)
        inner = (jax.nn.silu(dot(x, wg[e])) * dot(x, wu[e])).astype(BF16)
        ys[window, :] = dot(inner, wd[e]).astype(BF16)
        return carry
    for i in range(LOCAL // chunk):
        for copy in weights[3 * i:3 * i + 3]:
            copy.wait()
        lax.fori_loop(i * chunk, (i + 1) * chunk, experts, 0)

    for dz, dy, dc in others:
        gate_copy(dz, dy, dc).wait_send()
        s = slot(lax.rem(z + dz, NZ), dy, dc)
        remote(gate_ref, gates.at[s], gsem_s.at[0], gsem_r.at[s], at(z, 0, 1)).wait_recv()

    side = z // 2
    near = z - side * (2 * z - 3)
    order = []
    for i in range(NZ):
        value = (3, 2, 1 - near, near)[i]
        order.append(value + side * (3 - 2 * value))

    def weighted(s):
        ids = ids_ref[source(s)]
        gate = gates[s]
        g = jnp.zeros((LOCAL, TOK), F32)
        for k in range(TOP):
            g = g + jnp.where(expert == ids[k:k + 1, :], gate[k:k + 1, :], 0.0)
        jp = jpos[s]
        acc = jnp.zeros((TOK, TOK), F32)
        for e in range(LOCAL):
            acc = acc + jnp.where(sub == jp[e:e + 1, :], g[e:e + 1, :], 0.0)
        return split3(acc.T)

    def core_copy(zd, dy):
        i = zd * 2 + dy
        return remote(far_part.at[i], core_in.at[i], rc_s.at[i], rc_r.at[i], at(z, 0, 1))

    def y_copy(zd, half):
        part = pl.ds(half * HALF, HALF)
        return remote(own_part.at[zd * 2 + 1, part], y_in.at[zd, part], ry_s.at[zd, half], ry_r.at[zd, half], at(z, 1, 0))

    def z_copy(zd, half, step):
        part = pl.ds(half * HALF, HALF)
        if step == 1:
            return remote(own_part.at[zd * 2, part], right_in.at[zd, part], rr_s.at[zd, half], rr_r.at[zd, half], at(z + 1, 0, 0))
        return remote(own_part.at[zd * 2, part], left_in.at[zd, part], rl_s.at[zd, half], rl_r.at[zd, half], at(z - 1, 0, 0))

    def z_wait(zd, half, step):
        part = pl.ds(half * HALF, HALF)
        if step == 1:
            remote(own_part.at[zd * 2, part], right_in.at[zd, part], rr_s.at[zd, half], rr_r.at[zd, half], at(z, 0, 1)).wait_recv()
        else:
            remote(own_part.at[zd * 2, part], left_in.at[zd, part], rl_s.at[zd, half], rl_r.at[zd, half], at(z, 0, 1)).wait_recv()

    def combine(i, carry):
        value = jnp.where(i == 0, order[0], jnp.where(i == 1, order[1], jnp.where(i == 2, order[2], order[3])))
        zd = value
        for dy in (1, 0):
            s = slot(zd, dy, 0)
            for r in range(2):
                for e in range(LOCAL):
                    pick[r * TOK:(r + 1) * TOK, e * TOK:(e + 1) * TOK] = (sub == tgt[s + 1 - r, e:e + 1, :]).astype(F32).astype(BF16)
            pairs = dot(pick[...], ys[...]).astype(BF16)
            for r, part in ((0, far_part), (1, own_part)):
                high, mid, low3 = weighted(s + 1 - r)
                mine = pairs[r * TOK:(r + 1) * TOK]
                part[zd * 2 + dy] = (dot(low3, mine) + dot(mid, mine)) + dot(high, mine)
                if r == 0:
                    core_copy(zd, dy).start()
        for dy in (1, 0):
            core_copy(zd, dy).wait_recv()
            for half in range(2):
                part = pl.ds(half * HALF, HALF)
                own_part[zd * 2 + dy, part] += core_in[zd * 2 + dy, part]
                if dy == 1:
                    y_copy(zd, half).start()
        return carry

    lax.fori_loop(0, NZ, combine, 0)

    for i in range(NZ):
        zd = order[i]
        for half in range(2):
            part = pl.ds(half * HALF, HALF)
            y_copy(zd, half).wait_recv()
            own_part[zd * 2, part] += y_in[zd, part]
            if i < NZ - 1:
                @pl.when(zd > z)
                def _():
                    @pl.when(z > 0)
                    def _():
                        z_wait(zd, half, 1)
                        own_part[zd * 2, part] += right_in[zd, part]
                    z_copy(zd, half, 1).start()

                @pl.when(zd < z)
                def _():
                    @pl.when(z < NZ - 1)
                    def _():
                        z_wait(zd, half, -1)
                        own_part[zd * 2, part] += left_in[zd, part]
                    z_copy(zd, half, -1).start()
            else:
                @pl.when(z > 0)
                def _():
                    z_wait(z, half, 1)
                    own_part[z * 2, part] += right_in[z, part]

                @pl.when(z < NZ - 1)
                def _():
                    z_wait(z, half, -1)
                    own_part[z * 2, part] += left_in[z, part]
                out_ref[part, :] = (a_ref[part, :].astype(F32) + own_part[z * 2, part]).astype(BF16)

    own_to_core().wait_send()
    for half in range(2):
        own_to_y(half).wait_send()

        @pl.when(z < NZ - 1)
        def _():
            own_to_z(half, 1).wait_send()

        @pl.when(z > 0)
        def _():
            own_to_z(half, -1).wait_send()
    for k in range(1, NZ):
        zz = lax.rem(z + k, NZ)
        to_core(zz, 0).wait_send()
        for half in range(2):
            to_y(zz, half).wait_send()

            @pl.when((zz < z) & (z < NZ - 1))
            def _():
                to_z(zz, half, 1).wait_send()

            @pl.when((zz > z) & (z > 0))
            def _():
                to_z(zz, half, -1).wait_send()
    for zz in range(NZ):
        to_core(zz, 1).wait_send()
        for dy in range(2):
            core_copy(zz, dy).wait_send()
        for half in range(2):
            y_copy(zz, half).wait_send()

            @pl.when(zz > z)
            def _():
                z_copy(zz, half, 1).wait_send()

            @pl.when(zz < z)
            def _():
                z_copy(zz, half, -1).wait_send()


def moe(layer, u, gates, ids_all, a, wg, wu, wd):
    vmem = pl.BlockSpec(memory_space=pltpu.VMEM)
    hbm = pl.BlockSpec(memory_space=pl.ANY)
    sem = pltpu.SemaphoreType.DMA
    return pl.pallas_call(
        functools.partial(moe_kernel, layer),
        out_shape=jax.ShapeDtypeStruct((TOK, D), BF16),
        in_specs=[vmem, vmem, vmem, vmem, hbm, hbm, hbm],
        out_specs=vmem,
        scratch_shapes=[
            pltpu.VMEM((LOCAL, D, FF), BF16), pltpu.VMEM((LOCAL, D, FF), BF16), pltpu.VMEM((LOCAL, FF, D), BF16),
            pltpu.VMEM((NZ * NY, 2 * TOK, D), BF16), pltpu.VMEM((GROUP, TOP, TOK), F32),
            pltpu.VMEM((GROUP, LOCAL, TOK), F32), pltpu.VMEM((GROUP, LOCAL, TOK), F32), pltpu.VMEM((GROUP, LOCAL, TOK), F32),
            pltpu.VMEM((SLOTS, D), F32), pltpu.VMEM((SLOTS, D), BF16), pltpu.VMEM((2 * TOK, SLOTS), BF16),
            pltpu.VMEM((NZ * NY, TOK, D), F32), pltpu.VMEM((NZ * NY, TOK, D), F32), pltpu.VMEM((NZ * NY, TOK, D), F32),
            pltpu.VMEM((NZ, TOK, D), F32), pltpu.VMEM((NZ, TOK, D), F32), pltpu.VMEM((NZ, TOK, D), F32),
            sem((3, 4)), sem((GROUP,)), sem((GROUP,)),
            sem((NZ, 2, 2)), sem((NZ, 2)), sem((NZ, 2)), sem((NZ, 2)), sem((NZ, 2)), sem((NZ, 2)),
            sem((NZ * NY,)), sem((NZ * NY,)), sem((NZ, 2)), sem((NZ, 2)), sem((NZ, 2)), sem((NZ, 2)), sem((NZ, 2)), sem((NZ, 2)),
        ],
        compiler_params=pltpu.CompilerParams(vmem_limit_bytes=VMEM_LIMIT, collective_id=layer, has_side_effects=True),
        name='moe',
    )(u, gates, ids_all, a, wg, wu, wd)


def solution(mesh):
    def device_step(hidden, k_cache, v_cache, lengths, w_query, w_key, w_value, w_out, w_router, expert_ids, w_gate, w_up, w_down):
        layers = expert_ids.shape[0]
        kc = k_cache.reshape(layers, TOK, SEQ * KV, HD)
        vc = v_cache.reshape(layers, TOK, SEQ * KV, HD)
        ids = jnp.swapaxes(expert_ids, 1, 2)
        ids_all = lax.all_gather(ids, GROUP_AXES)
        for layer in range(layers):
            a, u, gates = attention(layer, hidden, kc, vc, lengths[None], w_query, w_key, w_value, w_out, w_router, ids)
            hidden = moe(layer, u, gates, ids_all[:, layer], a, w_gate, w_up, w_down)
        return hidden

    cache_spec = P(None, BATCH_AXES, None, None, None)
    expert_spec = P(None, GROUP_AXES, None, None)
    in_specs = (P(BATCH_AXES, None), cache_spec, cache_spec, P(BATCH_AXES), P(), P(), P(), P(), P(), P(None, BATCH_AXES, None), expert_spec, expert_spec, expert_spec)
    return jax.shard_map(device_step, mesh=mesh, in_specs=in_specs, out_specs=P(BATCH_AXES, None), check_vma=False)
```

time: 695 us -> 262 us (0.38)
  the two profiles are of different devices: /device:TPU:15 before, /device:TPU:0 now
where the time goes in v1:
time: 262 us
  Pallas kernels  236 us (90%)
  blocking collectives  23.5 us (9%)
    pallas_call x2, Pallas kernels, moe(): pl.pallas_call(functools.partial(moe_kernel, layer), out_shape=jax.ShapeD...  209 us
    pallas_call x2, Pallas kernels, attention(): pl.pallas_call(functools.partial(attention_kernel, layer), out_shape=(jax...  27.4 us
    all_gather x1, blocking collectives, device_step(): ids_all = lax.all_gather(ids, GROUP_AXES)  23.5 us

profile of v1, /device:TPU:0, one launch (start us, length us, event | category | flops | bytes accessed | tf_op | source)
XLA Modules:
  0.0 262.2 jit_solution(2588246735471407743)
XLA Ops:
  0.0 23.5 %all-gather = s32[32,8,128]{2,1,0:T(8,128)S(1)} all-gather(s32[2,8,128]{2,1,0:T(8,128)} %bitcast.18), channel_id=2, replica_groups=mesh['dp'=2,'pool'=4,'ep'=4] {'pool','ep'}, dimensions={0}, use_global_device_ids=true | all-gather | bytes 139264 | tf_op jit(solution)/shard_map/all_gather | solution.py:526
  23.5 0.7 slice_bitcast_fusion
  24.1 13.7 %attention.2 = (bf16[128,896]{1,0:T(8,128)(2,1)}, bf16[128,896]{1,0:T(8,128)(2,1)}, f32[8,128]{1,0:T(8,128)}) custom-call(bf16[128,896]{1,0:T(8,128)(2,1)} %x_ref.1, bf16[2,128,128,128]{3,2,1,0:T(8,128)(2,1)} %bitcast.13, bf16[2,128,128,128]{3,2,1,0:T(8,128)(2,1)} %bitcast.15, s32[1,128]{1,0:T(1,128)} %bitcast.21, bf16[2,896,2048]{2,1,0:T(8,128)(2,1)} %wq_hbm.3, ...), custom_call_target="tpu_custom_call" | custom-call | tf_op jit(solution)/shard_map/attention/pallas_call | solution.py:137
  37.8 102.1 %moe.2.x_ref = bf16[128,896]{1,0:T(8,128)(2,1)} custom-call(bf16[128,896]{1,0:T(8,128)(2,1)} %get-tuple-element.11.u_ref, f32[8,128]{1,0:T(8,128)} %get-tuple-element.12.gate_ref, s32[16,8,128]{2,1,0:T(8,128)} %get-tuple-element.18.ids_ref, bf16[128,896]{1,0:T(8,128)(2,1)} %get-tuple-element.13.a_ref, bf16[2,16,896,256]{3,2,1,0:T(8,128)(2,1)} %wg_hbm.3, ...), custom_call_target="tpu_custom_call" | custom-call | tf_op jit(solution)/shard_map/moe/pallas_call | solution.py:499
  140.0 13.7 %attention.3 = (bf16[128,896]{1,0:T(8,128)(2,1)}, bf16[128,896]{1,0:T(8,128)(2,1)}, f32[8,128]{1,0:T(8,128)}) custom-call(bf16[128,896]{1,0:T(8,128)(2,1)} %moe.2.x_ref, bf16[2,128,128,128]{3,2,1,0:T(8,128)(2,1)} %bitcast.14, bf16[2,128,128,128]{3,2,1,0:T(8,128)(2,1)} %bitcast.16, s32[1,128]{1,0:T(1,128)} %bitcast.22, bf16[2,896,2048]{2,1,0:T(8,128)(2,1)} %wq_hbm.3, ...), custom_call_target="tpu_custom_call" | custom-call | tf_op jit(solution)/shard_map/attention/pallas_call | solution.py:137
  153.7 106.9 %moe.3 = bf16[128,896]{1,0:T(8,128)(2,1)} custom-call(bf16[128,896]{1,0:T(8,128)(2,1)} %get-tuple-element.14.u_ref, f32[8,128]{1,0:T(8,128)} %get-tuple-element.15.gate_ref, s32[16,8,128]{2,1,0:T(8,128)} %get-tuple-element.17.ids_ref, bf16[128,896]{1,0:T(8,128)(2,1)} %get-tuple-element.16.a_ref, bf16[2,16,896,256]{3,2,1,0:T(8,128)(2,1)} %wg_hbm.3, ...), custom_call_target="tpu_custom_call" | custom-call | tf_op jit(solution)/shard_map/moe/pallas_call | solution.py:499
  260.6 1.6 copy.21

commit v2 on v1

v2 whole, which is shorter than its diff:
```python
import functools

import jax
import jax.numpy as jnp
from jax import lax
from jax.experimental import pallas as pl
from jax.experimental.pallas import tpu as pltpu
from jax.sharding import PartitionSpec as P

EPS = 1e-6
GROUP_AXES = ('pool', 'ep')
BATCH_AXES = ('dp', 'pool', 'ep')
MESH = pl.DeviceIdType.MESH
F32 = jnp.float32
BF16 = jnp.bfloat16
VMEM_LIMIT = 66_000_000

NZ, NY = 4, 2
GROUP = 16
TOK = 128
HALF = TOK // 2
D = 896
HEADS, KV, HD, SEQ = 16, 4, 128, 32
PER_KV = HEADS // KV
TOP = 8
EXPERTS, LOCAL, FF = 256, 16, 256
SLOTS = LOCAL * TOK
BLK = 16


def rms(wide):
    return wide * lax.rsqrt(jnp.mean(wide * wide, axis=-1, keepdims=True) + EPS)


def dot(a, b):
    return jnp.dot(a, b, preferred_element_type=F32)


def split3(wide):
    high = wide.astype(BF16)
    rest = wide - high.astype(F32)
    mid = rest.astype(BF16)
    low = (rest - mid.astype(F32)).astype(BF16)
    return high, mid, low


OTHERS = [(dz, dy, dc) for dz in range(NZ) for dy in range(NY) for dc in range(2) if (dz, dy, dc) != (0, 0, 0)]


def position():
    z = lax.axis_index('pool')
    ep = lax.axis_index('ep')
    y = ep // 2
    core = lax.rem(ep, 2)

    def at(zz, dy, dc):
        return {'pool': zz, 'ep': lax.rem(y + dy, 2) * 2 + lax.rem(core + dc, 2)}
    return z, y, core, at


def slot(zz, dy, dc):
    return (zz * 2 + dy) * 2 + dc


def remote(src, dst, send, recv, target):
    return pltpu.make_async_remote_copy(src_ref=src, dst_ref=dst, send_sem=send, recv_sem=recv, device_id=target, device_id_type=MESH)


def attention_kernel(layer, x_ref, kc_hbm, vc_hbm, len_ref, wq_hbm, wk_hbm, wv_hbm, wo_hbm, wr_hbm, ids_ref, *refs):
    share = layer == 0
    if share:
        a_ref, u_ref, gate_ref, all_ref, wq, wk, wv, wo, wr, kc, vc, qs, ks, vs, os, mixed, wsem, ksem, vsem, held, send_sem, recv_sem = refs
    else:
        a_ref, u_ref, gate_ref, wq, wk, wv, wo, wr, kc, vc, qs, ks, vs, os, mixed, wsem, ksem, vsem = refs
    if share:
        z, y, core, at = position()
        barrier = pltpu.get_barrier_semaphore()
        for dz, dy, dc in OTHERS:
            pl.semaphore_signal(barrier, inc=1, device_id=at(lax.rem(z + dz, NZ), dy, dc), device_id_type=MESH)
    parts = 4
    step = TOK // parts
    loads = [pltpu.make_async_copy(src.at[layer], dst, wsem.at[i]) for i, (src, dst) in enumerate(
        ((wq_hbm, wq), (wk_hbm, wk), (wv_hbm, wv), (wo_hbm, wo), (wr_hbm, wr)))]
    k_loads = [pltpu.make_async_copy(kc_hbm.at[layer, pl.ds(i * step, step)], kc.at[pl.ds(i * step, step)], ksem.at[i]) for i in range(parts)]
    v_loads = [pltpu.make_async_copy(vc_hbm.at[layer, pl.ds(i * step, step)], vc.at[pl.ds(i * step, step)], vsem.at[i]) for i in range(parts)]
    for copy in loads[:3]:
        copy.start()
    for i in range(parts):
        k_loads[i].start()
        v_loads[i].start()
    for copy in loads[3:]:
        copy.start()
    if share:
        pl.semaphore_wait(barrier, len(OTHERS))
        sends = []
        for dz, dy, dc in OTHERS:
            sends.append(remote(ids_ref, held.at[slot(z, dy, dc)], send_sem.at[dz * 4 + dy * 2 + dc], recv_sem.at[slot(z, dy, dc)], at(lax.rem(z + dz, NZ), dy, dc)))
            sends[-1].start()
        held[slot(z, 0, 0)] = ids_ref[...]

    x = x_ref[...].astype(F32)
    h = rms(x).astype(BF16)
    loads[0].wait()
    for c in range(4):
        q = dot(h, wq[:, c * 512:(c + 1) * 512]).astype(BF16).astype(F32)
        for j in range(4):
            qs[pl.ds(c * 4 + j, TOK, stride=HEADS), :] = q[:, j * HD:(j + 1) * HD]
    loads[1].wait()
    k_new = dot(h, wk[...]).astype(BF16).astype(F32)
    loads[2].wait()
    v_new = dot(h, wv[...]).astype(BF16).astype(F32)
    for i in range(HEADS):
        j = i // PER_KV
        ks[pl.ds(i, TOK, stride=HEADS), :] = k_new[:, j * HD:(j + 1) * HD]
        vs[pl.ds(i, TOK, stride=HEADS), :] = v_new[:, j * HD:(j + 1) * HD]

    scale = HD ** -0.5
    lane = lax.broadcasted_iota(jnp.int32, (HEADS, SEQ * KV), 1)
    head = lax.broadcasted_iota(jnp.int32, (HEADS, SEQ * KV), 0)
    own_kv = lax.rem(lane, KV) == head // PER_KV
    pos = jnp.where(own_kv, lane // KV, SEQ)

    def attend(b, carry):
        tok = b * BLK
        rows = pl.ds(tok * HEADS, BLK * HEADS)
        q_wide = qs[rows, :]
        q_blk = q_wide.astype(BF16)
        score_list, mask_list = [], []
        for t in range(BLK):
            score_list.append(lax.dot_general(q_blk[t * HEADS:(t + 1) * HEADS], kc[tok + t], (((1,), (1,)), ((), ())), preferred_element_type=F32))
            mask_list.append(pos < len_ref[0, tok + t])
        score = jnp.concatenate(score_list, axis=0) * scale
        mask = jnp.concatenate(mask_list, axis=0)
        score = jnp.where(mask, score, -jnp.inf)
        score_new = jnp.sum(q_wide * ks[rows, :], axis=-1, keepdims=True) * scale
        peak = jnp.maximum(jnp.max(score, axis=-1, keepdims=True), score_new)
        prob = jnp.exp(score - peak)
        prob_new = jnp.exp(score_new - peak)
        total = jnp.sum(prob, axis=-1, keepdims=True) + prob_new
        prob = (prob / total).astype(BF16)
        prob_new = (prob_new / total).astype(BF16).astype(F32)
        out = [dot(prob[t * HEADS:(t + 1) * HEADS], vc[tok + t]) for t in range(BLK)]
        out = jnp.concatenate(out, axis=0) + prob_new * vs[rows, :]
        os[rows, :] = out.astype(BF16).astype(F32)
        return carry

    per_part = step // BLK
    for i in range(parts):
        k_loads[i].wait()
        v_loads[i].wait()
        lax.fori_loop(i * per_part, (i + 1) * per_part, attend, 0)

    for i in range(HEADS):
        mixed[:, i * HD:(i + 1) * HD] = os[pl.ds(i, TOK, stride=HEADS), :].astype(BF16)
    loads[3].wait()
    a = (x + dot(mixed[...], wo[...])).astype(BF16)
    a_ref[...] = a
    u = rms(a.astype(F32)).astype(BF16)
    u_ref[...] = u
    loads[4].wait()
    high, mid, low = split3(wr[...])
    logits = (dot(u, low) + dot(u, mid)) + dot(u, high)
    logits = logits.T
    expert = lax.broadcasted_iota(jnp.int32, (EXPERTS, TOK), 0)
    chosen = [jnp.sum(jnp.where(expert == ids_ref[layer, k:k + 1, :], logits, 0.0), axis=0, keepdims=True) for k in range(TOP)]
    chosen = jnp.concatenate(chosen, axis=0)
    weight = jnp.exp(chosen - jnp.max(chosen, axis=0, keepdims=True))
    gate_ref[...] = weight / jnp.sum(weight, axis=0, keepdims=True)
    if share:
        for copy, (dz, dy, dc) in zip(sends, OTHERS):
            i = slot(lax.rem(z + dz, NZ), dy, dc)
            copy.wait_send()
            remote(ids_ref, held.at[i], send_sem.at[0], recv_sem.at[i], at(z, 0, 1)).wait_recv()
        all_ref[...] = held[...]


def attention(layer, hidden, kc, vc, lengths, wq, wk, wv, wo, wr, ids):
    vmem = pl.BlockSpec(memory_space=pltpu.VMEM)
    hbm = pl.BlockSpec(memory_space=pl.ANY)
    out_shape = (jax.ShapeDtypeStruct((TOK, D), BF16), jax.ShapeDtypeStruct((TOK, D), BF16), jax.ShapeDtypeStruct((TOP, TOK), F32))
    params = dict(vmem_limit_bytes=VMEM_LIMIT)
    extra = []
    if layer == 0:
        out_shape += (jax.ShapeDtypeStruct((GROUP,) + ids.shape, jnp.int32),)
        extra = [pltpu.VMEM((GROUP,) + ids.shape, jnp.int32), pltpu.SemaphoreType.DMA((GROUP,)), pltpu.SemaphoreType.DMA((GROUP,))]
        params.update(collective_id=2, has_side_effects=True)
    return pl.pallas_call(
        functools.partial(attention_kernel, layer),
        out_shape=out_shape,
        in_specs=[vmem, hbm, hbm, pl.BlockSpec(memory_space=pltpu.SMEM), hbm, hbm, hbm, hbm, hbm, vmem],
        out_specs=(vmem,) * len(out_shape),
        scratch_shapes=[
            pltpu.VMEM((D, HEADS * HD), BF16), pltpu.VMEM((D, KV * HD), BF16), pltpu.VMEM((D, KV * HD), BF16),
            pltpu.VMEM((HEADS * HD, D), BF16), pltpu.VMEM((D, EXPERTS), F32),
            pltpu.VMEM((TOK, SEQ * KV, HD), BF16), pltpu.VMEM((TOK, SEQ * KV, HD), BF16),
            pltpu.VMEM((TOK * HEADS, HD), F32), pltpu.VMEM((TOK * HEADS, HD), F32), pltpu.VMEM((TOK * HEADS, HD), F32),
            pltpu.VMEM((TOK * HEADS, HD), F32), pltpu.VMEM((TOK, HEADS * HD), BF16),
            pltpu.SemaphoreType.DMA((5,)), pltpu.SemaphoreType.DMA((4,)), pltpu.SemaphoreType.DMA((4,)),
        ] + extra,
        compiler_params=pltpu.CompilerParams(**params),
        name='attention',
    )(hidden, kc, vc, lengths, wq, wk, wv, wo, wr, ids)


EDGE = 16
GATHER = ((0, 80), (80, 48))
REDUCE = ((0, EDGE), (EDGE, 56), (72, 56))


def moe_kernel(layer, u_ref, gate_ref, ids_ref, a_ref, wg_hbm, wu_hbm, wd_hbm, out_ref,
               wg, wu, wd, rows, gates, pos, jpos, tgt, xs, ys, pick,
               core_in, y_in, y_edge, right_in, right_edge, left_in, left_edge,
               wsem, gsem_s, gsem_r, az_s, az_r, ay_s, ay_r, ac_s, ac_r,
               rc_s, rc_r, ry_s, ry_r, rr_s, rr_r, rl_s, rl_r):
    z, y, core, at = position()
    first = (z * 4 + y * 2 + core) * LOCAL
    side = z // 2
    near = z - side * (2 * z - 3)
    mirror = lambda v: v + side * (3 - 2 * v)
    n1, n2, n3 = mirror(1 - near), mirror(2), mirror(3)
    order = (mirror(3), mirror(2), mirror(1 - near), mirror(near))

    barrier = pltpu.get_barrier_semaphore()
    for dz, dy, dc in OTHERS:
        pl.semaphore_signal(barrier, inc=1, device_id=at(lax.rem(z + dz, NZ), dy, dc), device_id_type=MESH)

    chunk = 4
    weights = []
    for i in range(LOCAL // chunk):
        part = pl.ds(i * chunk, chunk)
        for j, (src, dst) in enumerate(((wg_hbm, wg), (wu_hbm, wu), (wd_hbm, wd))):
            weights.append(pltpu.make_async_copy(src.at[layer, part], dst.at[part], wsem.at[j, i]))
    for copy in weights:
        copy.start()

    expert = lax.broadcasted_iota(jnp.int32, (LOCAL, TOK), 0) + first
    tri = (lax.broadcasted_iota(jnp.int32, (TOK, TOK), 0) < lax.broadcasted_iota(jnp.int32, (TOK, TOK), 1)).astype(BF16)
    ones = jnp.ones((TOK, TOK), BF16)
    low = (lax.broadcasted_iota(jnp.int32, (LOCAL, LOCAL), 1) < lax.broadcasted_iota(jnp.int32, (LOCAL, LOCAL), 0)).astype(BF16)
    lane = lax.broadcasted_iota(jnp.int32, (LOCAL, TOK), 1).astype(F32)
    sub = lax.broadcasted_iota(jnp.int32, (TOK, TOK), 0).astype(F32)

    def plan(s, base):
        ids = ids_ref[s, layer]
        hit = jnp.zeros((LOCAL, TOK), F32)
        for k in range(TOP):
            hit = hit + jnp.where(expert == ids[k:k + 1, :], 1.0, 0.0)
        hit16 = hit.astype(BF16)
        rank = dot(hit16, tri)
        count = dot(hit16, ones)
        offset = dot(low, count.astype(BF16))
        pos[s] = jnp.where(hit > 0, base + rank, -1.0)
        jpos[s] = jnp.where(hit > 0, offset + rank, -1.0)
        local = lane - base
        tgt[s] = jnp.where((local >= 0) & (local < count), local + offset, -1.0)
        return base + count

    with jax.named_scope('plan'):
        lax.fori_loop(0, GROUP, plan, jnp.zeros((LOCAL, TOK), F32), unroll=2)

    with jax.named_scope('barrier'):
        pl.semaphore_wait(barrier, len(OTHERS))

    def block(zz, dy, dc, start, count):
        return rows.at[zz * 2 + dy, pl.ds(dc * TOK + start, count)]

    def z_send(zz, c, step):
        if c == 2:
            src = block(zz, 1, 0, 0, EDGE)
        else:
            src = block(zz, 0, 0, *GATHER[c])
        return remote(src, src, az_s.at[zz, c, (step + 1) // 2], az_r.at[zz, c], at(z + step, 0, 0))

    def own_z_send(c, step):
        return remote(u_ref.at[pl.ds(*GATHER[c])], block(z, 0, 0, *GATHER[c]), az_s.at[z, c, (step + 1) // 2], az_r.at[z, c], at(z + step, 0, 0))

    def z_arrival(zz, c):
        src = block(zz, 1, 0, 0, EDGE) if c == 2 else block(zz, 0, 0, *GATHER[c])
        return remote(src, src, az_s.at[zz, c, 0], az_r.at[zz, c], at(z, 0, 1))

    def y_piece(c):
        start, count = GATHER[c]
        return (EDGE, count - EDGE) if c == 0 else (start, count)

    def y_send(zz, c):
        return remote(block(zz, 0, 0, *y_piece(c)), block(zz, 1, 0, *y_piece(c)), ay_s.at[zz, c], ay_r.at[zz, c], at(z, 1, 0))

    def own_y_send(c):
        return remote(u_ref.at[pl.ds(*GATHER[c])], block(z, 1, 0, *GATHER[c]), ay_s.at[z, c], ay_r.at[z, c], at(z, 1, 0))

    def core_send(zz, dy):
        return remote(block(zz, dy, 0, 0, TOK), block(zz, dy, 1, 0, TOK), ac_s.at[zz, dy], ac_r.at[zz, dy], at(z, 0, 1))

    def own_core_send():
        return remote(u_ref, block(z, 0, 1, 0, TOK), ac_s.at[z, 0], ac_r.at[z, 0], at(z, 0, 1))

    def both_ways(make, act):
        @pl.when(z < NZ - 1)
        def _():
            getattr(make(1), act)()

        @pl.when(z > 0)
        def _():
            getattr(make(-1), act)()

    def onward(zz, c, act):
        @pl.when((zz < z) & (z < NZ - 1))
        def _():
            getattr(z_send(zz, c, 1), act)()

        @pl.when((zz > z) & (z > 0))
        def _():
            getattr(z_send(zz, c, -1), act)()

    own_core_send().start()
    for c in range(2):
        both_ways(lambda step: own_z_send(c, step), 'start')
        own_y_send(c).start()

    def gate_copy(dz, dy, dc):
        me = slot(z, dy, dc)
        return remote(gate_ref, gates.at[me], gsem_s.at[dz * 4 + dy * 2 + dc], gsem_r.at[me], at(lax.rem(z + dz, NZ), dy, dc))

    for o in OTHERS:
        gate_copy(*o).start()
    gates[slot(z, 0, 0)] = gate_ref[...]
    rows[z * 2, pl.ds(0, TOK), :] = u_ref[...]

    per = 4

    def fill(zz, dy, fresh=False):
        chip = zz * 2 + dy

        def body(i, carry):
            picks = []
            for j in range(per):
                e = i * per + j
                picks.append(jnp.concatenate([(sub == pos[chip * 2 + dc, pl.ds(e, 1), :]).astype(F32).astype(BF16) for dc in range(2)], axis=1))
            got = dot(jnp.concatenate(picks, axis=0), rows[chip])
            where = pl.ds(pl.multiple_of(i * per * TOK, per * TOK), per * TOK)
            if fresh:
                xs[where, :] = got
            else:
                xs[where, :] += got
            return carry
        with jax.named_scope('fill'):
            core_send(zz, dy).wait_recv()
            lax.fori_loop(0, LOCAL // per, body, 0)

    def arrive(zz, c):
        z_arrival(zz, c).wait_recv()
        onward(zz, c, 'start')
        if c < 2:
            y_send(zz, c).start()
        if c == 1:
            core_send(zz, 0).start()

    def arrive_y(zz):
        for c in range(2):
            y_send(zz, c).wait_recv()
        core_send(zz, 1).start()

    inside, end = near == 1, near == 0
    fill(z, 0, True)
    arrive(n1, 0)
    pl.when(inside)(lambda: arrive(n2, 0))
    own_y_send(0).wait_recv()
    both_ways(lambda step: z_send(z, 2, step), 'start')
    arrive(n1, 1)
    pl.when(inside)(lambda: arrive(n2, 1))
    own_y_send(1).wait_recv()
    core_send(z, 1).start()
    fill(n1, 0)
    pl.when(end)(lambda: arrive(n2, 0))
    pl.when(inside)(lambda: arrive(n3, 0))
    arrive(n1, 2)
    pl.when(inside)(lambda: arrive(n2, 2))
    fill(z, 1)
    pl.when(end)(lambda: arrive(n2, 1))
    pl.when(inside)(lambda: arrive(n3, 1))
    fill(n2, 0)
    pl.when(end)(lambda: arrive(n2, 2))
    pl.when(end)(lambda: arrive(n3, 0))
    arrive_y(n1)
    fill(n1, 1)
    pl.when(end)(lambda: arrive(n3, 1))
    arrive_y(n2)
    fill(n3, 0)
    arrive(n3, 2)
    fill(n2, 1)
    arrive_y(n3)
    fill(n3, 1)

    def experts(e, carry):
        window = pl.ds(pl.multiple_of(e * TOK, TOK), TOK)
        x = xs[window, :].astype(BF16)
        inner = (jax.nn.silu(dot(x, wg[e])) * dot(x, wu[e])).astype(BF16)
        ys[window, :] = dot(inner, wd[e]).astype(BF16)
        return carry
    with jax.named_scope('experts'):
        for i in range(LOCAL // chunk):
            for copy in weights[3 * i:3 * i + 3]:
                copy.wait()
            lax.fori_loop(i * chunk, (i + 1) * chunk, experts, 0)

    for dz, dy, dc in OTHERS:
        gate_copy(dz, dy, dc).wait_send()
        s = slot(lax.rem(z + dz, NZ), dy, dc)
        remote(gate_ref, gates.at[s], gsem_s.at[0], gsem_r.at[s], at(z, 0, 1)).wait_recv()

    def own_part(i, start=0, count=TOK):
        return xs.at[pl.ds(pl.multiple_of(i * TOK + start, 8), count)]

    def far_part(i):
        return xs.at[pl.ds(pl.multiple_of((NZ * NY + i) * TOK, TOK), TOK)]

    def weighted(s):
        ids = ids_ref[s, layer]
        gate = gates[s]
        g = jnp.zeros((LOCAL, TOK), F32)
        for k in range(TOP):
            g = g + jnp.where(expert == ids[k:k + 1, :], gate[k:k + 1, :], 0.0)
        jp = jpos[s]
        acc = jnp.zeros((TOK, TOK), F32)
        for e in range(LOCAL):
            acc = acc + jnp.where(sub == jp[e:e + 1, :], g[e:e + 1, :], 0.0)
        return split3(acc.T)

    def core_copy(i):
        return remote(far_part(i), core_in.at[i], rc_s.at[i], rc_r.at[i], at(z, 0, 1))

    def y_copy(zd, c):
        part = pl.ds(*REDUCE[c])
        if c == 0:
            dst = y_edge
        else:
            dst = y_in.at[zd, part]
        return remote(own_part(zd * 2 + 1, *REDUCE[c]), dst, ry_s.at[zd, c], ry_r.at[zd, c], at(z, 1, 0))

    def z_copy(zd, c, step, target=None):
        main, edge, send, recv = (right_in, right_edge, rr_s, rr_r) if step == 1 else (left_in, left_edge, rl_s, rl_r)
        target = at(z + step, 0, 0) if target is None else target
        if c == 3:
            return remote(own_part(zd * 2 + 1, 0, EDGE), edge.at[zd], send.at[zd, c], recv.at[zd, c], target)
        return remote(own_part(zd * 2, *REDUCE[c]), main.at[zd, pl.ds(*REDUCE[c])], send.at[zd, c], recv.at[zd, c], target)

    def take(zd, c, step):
        z_copy(zd, c, step, at(z, 0, 1)).wait_recv()
        main, edge = (right_in, right_edge) if step == 1 else (left_in, left_edge)
        if c == 3:
            own_part(zd * 2 + 1, 0, EDGE)[...] += edge[zd]
        else:
            own_part(zd * 2, *REDUCE[c])[...] += main[zd, pl.ds(*REDUCE[c])]

    def chain(zd, c):
        @pl.when(zd > z)
        def _():
            @pl.when(z > 0)
            def _():
                take(zd, c, 1)
            z_copy(zd, c, 1).start()

        @pl.when(zd < z)
        def _():
            @pl.when(z < NZ - 1)
            def _():
                take(zd, c, -1)
            z_copy(zd, c, -1).start()

    def last(c):
        @pl.when(z > 0)
        def _():
            take(z, c, 1)

        @pl.when(z < NZ - 1)
        def _():
            take(z, c, -1)

    def cross(zd, c):
        y_copy(zd, c).wait_recv()
        own_part(zd * 2, *REDUCE[c])[...] += y_in[zd, pl.ds(*REDUCE[c])]

    def edges(zd):
        chain(zd, 0)
        chain(zd, 3)

    def piece(zd, c):
        cross(zd, c)
        chain(zd, c)

    steps = ((0, 1), (1, 1), (0, 0), (2, 1), (1, 0), (3, 1), (2, 0), (3, 0))
    targets = [order[i] * 2 + dy for i, dy in steps]

    def pick_target(j):
        value = targets[0]
        for i in range(1, len(steps)):
            value = jnp.where(j == i, targets[i], value)
        return value

    def finish(j):
        i = pick_target(j)
        core_copy(i).wait_recv()
        own_part(i)[...] += core_in[i]

        @pl.when(lax.rem(i, 2) == 1)
        def _():
            for c in (1, 2):
                y_copy(i // 2, c).start()

    def combine(j, carry):
        i = pick_target(j)
        s = i * 2
        for r in range(2):
            for e in range(LOCAL):
                pick[r * TOK:(r + 1) * TOK, e * TOK:(e + 1) * TOK] = (sub == tgt[s + 1 - r, e:e + 1, :]).astype(F32).astype(BF16)
        pairs = dot(pick[...], ys[...]).astype(BF16)
        for r, part in ((0, far_part), (1, own_part)):
            high, mid, low3 = weighted(s + 1 - r)
            mine = pairs[r * TOK:(r + 1) * TOK]
            part(i)[...] = (dot(low3, mine) + dot(mid, mine)) + dot(high, mine)
            if r == 0:
                core_copy(i).start()

        @pl.when(j > 0)
        def _():
            finish(j - 1)

        @pl.when(end & (j == 4))
        def _():
            edges(order[0])
            piece(order[0], 1)

        @pl.when(end & (j == 5))
        def _():
            piece(order[0], 2)

        @pl.when(end & (j == 7))
        def _():
            edges(order[1])
            piece(order[1], 1)
        return carry

    with jax.named_scope('combine'):
        lax.fori_loop(0, len(steps), combine, 0)

    with jax.named_scope('chain'):
        finish(len(steps) - 1)

        @pl.when(inside)
        def _():
            edges(order[0])
            piece(order[0], 1)
            piece(order[0], 2)
            edges(order[1])
            piece(order[1], 1)
        piece(order[1], 2)
        edges(order[2])
        piece(order[2], 1)
        last(3)
        y_copy(z, 0).start()
        piece(order[2], 2)
        last(0)
        for c in (1, 2):
            cross(z, c)
            last(c)
        y_copy(z, 0).wait_recv()
        own_part(z * 2, 0, EDGE)[...] += y_edge[...]
        out_ref[...] = (a_ref[...].astype(F32) + own_part(z * 2)[...]).astype(BF16)

    own_core_send().wait_send()
    for c in range(2):
        own_y_send(c).wait_send()
        both_ways(lambda step: own_z_send(c, step), 'wait_send')
    both_ways(lambda step: z_send(z, 2, step), 'wait_send')
    for zz in (n1, n2, n3):
        core_send(zz, 0).wait_send()
        for c in range(3):
            onward(zz, c, 'wait_send')
            if c < 2:
                y_send(zz, c).wait_send()
    for zz in range(NZ):
        core_send(zz, 1).wait_send()
        for dy in range(2):
            core_copy(zz * 2 + dy).wait_send()
        for c in (1, 2):
            y_copy(zz, c).wait_send()
        for c in range(4):
            @pl.when(zz > z)
            def _():
                z_copy(zz, c, 1).wait_send()

            @pl.when(zz < z)
            def _():
                z_copy(zz, c, -1).wait_send()
    y_copy(z, 0).wait_send()


def moe(layer, u, gates, ids_all, a, wg, wu, wd):
    vmem = pl.BlockSpec(memory_space=pltpu.VMEM)
    hbm = pl.BlockSpec(memory_space=pl.ANY)
    sem = pltpu.SemaphoreType.DMA
    return pl.pallas_call(
        functools.partial(moe_kernel, layer),
        out_shape=jax.ShapeDtypeStruct((TOK, D), BF16),
        in_specs=[vmem, vmem, vmem, vmem, hbm, hbm, hbm],
        out_specs=vmem,
        scratch_shapes=[
            pltpu.VMEM((LOCAL, D, FF), BF16), pltpu.VMEM((LOCAL, D, FF), BF16), pltpu.VMEM((LOCAL, FF, D), BF16),
            pltpu.VMEM((NZ * NY, 2 * TOK, D), BF16), pltpu.VMEM((GROUP, TOP, TOK), F32),
            pltpu.VMEM((GROUP, LOCAL, TOK), F32), pltpu.VMEM((GROUP, LOCAL, TOK), F32), pltpu.VMEM((GROUP, LOCAL, TOK), F32),
            pltpu.VMEM((SLOTS, D), F32), pltpu.VMEM((SLOTS, D), BF16), pltpu.VMEM((2 * TOK, SLOTS), BF16),
            pltpu.VMEM((NZ * NY, TOK, D), F32), pltpu.VMEM((NZ, TOK, D), F32), pltpu.VMEM((EDGE, D), F32),
            pltpu.VMEM((NZ, TOK, D), F32), pltpu.VMEM((NZ, EDGE, D), F32), pltpu.VMEM((NZ, TOK, D), F32), pltpu.VMEM((NZ, EDGE, D), F32),
            sem((3, 4)), sem((GROUP,)), sem((GROUP,)),
            sem((NZ, 3, 2)), sem((NZ, 3)), sem((NZ, 2)), sem((NZ, 2)), sem((NZ, 2)), sem((NZ, 2)),
            sem((NZ * NY,)), sem((NZ * NY,)), sem((NZ, 3)), sem((NZ, 3)), sem((NZ, 4)), sem((NZ, 4)), sem((NZ, 4)), sem((NZ, 4)),
        ],
        compiler_params=pltpu.CompilerParams(vmem_limit_bytes=VMEM_LIMIT, collective_id=layer, has_side_effects=True),
        name='moe',
    )(u, gates, ids_all, a, wg, wu, wd)


def solution(mesh):
    def device_step(hidden, k_cache, v_cache, lengths, w_query, w_key, w_value, w_out, w_router, expert_ids, w_gate, w_up, w_down):
        layers = expert_ids.shape[0]
        kc = k_cache.reshape(layers, TOK, SEQ * KV, HD)
        vc = v_cache.reshape(layers, TOK, SEQ * KV, HD)
        ids = jnp.swapaxes(expert_ids, 1, 2)
        for layer in range(layers):
            a, u, gates, *shared = attention(layer, hidden, kc, vc, lengths[None], w_query, w_key, w_value, w_out, w_router, ids)
            if shared:
                ids_all = shared[0]
            hidden = moe(layer, u, gates, ids_all, a, w_gate, w_up, w_down)
        return hidden

    cache_spec = P(None, BATCH_AXES, None, None, None)
    expert_spec = P(None, GROUP_AXES, None, None)
    in_specs = (P(BATCH_AXES, None), cache_spec, cache_spec, P(BATCH_AXES), P(), P(), P(), P(), P(), P(None, BATCH_AXES, None), expert_spec, expert_spec, expert_spec)
    return jax.shard_map(device_step, mesh=mesh, in_specs=in_specs, out_specs=P(BATCH_AXES, None), check_vma=False)
```

time: 262 us -> 217 us (0.83)
  blocking collectives: 23.5 us -> 0 us
  Pallas kernels: 236 us -> 215 us
    pallas_call x2, Pallas kernels: 209 us -> 183 us  [moe(): pl.pallas_call(functools.partial(moe_kernel, layer), out_shape=jax.ShapeD...]
    all_gather x1 -> x0, blocking collectives: 23.5 us -> none  [device_step(): ids_all = lax.all_gather(ids, GROUP_AXES)]
    pallas_call x2, Pallas kernels: 27.4 us -> 32.2 us  [attention(): pl.pallas_call(functools.partial(attention_kernel, layer), out_shape=out_...]
where the time goes in v2:
time: 217 us
  Pallas kernels  215 us (99%)
    pallas_call x2, Pallas kernels, moe(): pl.pallas_call(functools.partial(moe_kernel, layer), out_shape=jax.ShapeD...  183 us
    pallas_call x2, Pallas kernels, attention(): pl.pallas_call(functools.partial(attention_kernel, layer), out_shape=out_...  32.2 us

profile of v2, /device:TPU:0, one launch (start us, length us, event | category | flops | bytes accessed | tf_op | source)
XLA Modules:
  0.0 216.6 jit_solution(6959162814361676384)
XLA Ops:
  0.0 18.5 %attention.2 = (bf16[128,896]{1,0:T(8,128)(2,1)}, bf16[128,896]{1,0:T(8,128)(2,1)}, f32[8,128]{1,0:T(8,128)}, s32[16,2,8,128]{3,2,1,0:T(8,128)}) custom-call(bf16[128,896]{1,0:T(8,128)(2,1)} %x_ref.1, bf16[2,128,128,128]{3,2,1,0:T(8,128)(2,1)} %bitcast.4, bf16[2,128,128,128]{3,2,1,0:T(8,128)(2,1)} %bitcast.6, s32[1,128]{1,0:T(1,128)} %bitcast.10, ...), custom_call_target="tpu_custom_call" | custom-call | tf_op jit(solution)/shard_map/attention/pallas_call | solution.py:187
  18.5 91.8 %moe.2.x_ref = bf16[128,896]{1,0:T(8,128)(2,1)} custom-call(bf16[128,896]{1,0:T(8,128)(2,1)} %get-tuple-element.12.u_ref, f32[8,128]{1,0:T(8,128)} %get-tuple-element.13.gate_ref, s32[16,2,8,128]{3,2,1,0:T(8,128)} %get-tuple-element.14.ids_ref, bf16[128,896]{1,0:T(8,128)(2,1)} %get-tuple-element.15.a_ref, bf16[2,16,896,256]{3,2,1,0:T(8,128)(2,1)} %wg_hbm.3, ...), custom_call_target="tpu_custom_call" | custom-call | tf_op jit(solution)/shard_map/moe/pallas_call | solution.py:602
  110.3 13.7 %attention.3 = (bf16[128,896]{1,0:T(8,128)(2,1)}, bf16[128,896]{1,0:T(8,128)(2,1)}, f32[8,128]{1,0:T(8,128)}) custom-call(bf16[128,896]{1,0:T(8,128)(2,1)} %moe.2.x_ref, bf16[2,128,128,128]{3,2,1,0:T(8,128)(2,1)} %bitcast.5, bf16[2,128,128,128]{3,2,1,0:T(8,128)(2,1)} %bitcast.7, s32[1,128]{1,0:T(1,128)} %bitcast.11, bf16[2,896,2048]{2,1,0:T(8,128)(2,1)} %wq_hbm.3, ...), custom_call_target="tpu_custom_call" | custom-call | tf_op jit(solution)/shard_map/attention/pallas_call | solution.py:187
  124.0 90.9 %moe.3 = bf16[128,896]{1,0:T(8,128)(2,1)} custom-call(bf16[128,896]{1,0:T(8,128)(2,1)} %get-tuple-element.16.u_ref, f32[8,128]{1,0:T(8,128)} %get-tuple-element.17.gate_ref, s32[16,2,8,128]{3,2,1,0:T(8,128)} %get-tuple-element.14.ids_ref, bf16[128,896]{1,0:T(8,128)(2,1)} %get-tuple-element.18.a_ref, bf16[2,16,896,256]{3,2,1,0:T(8,128)(2,1)} %wg_hbm.3, ...), custom_call_target="tpu_custom_call" | custom-call | tf_op jit(solution)/shard_map/moe/pallas_call | solution.py:602
  215.0 1.6 copy.15

commit v3 on v2

v3 whole, which is shorter than its diff:
```python
import functools

import jax
import jax.numpy as jnp
from jax import lax
from jax.experimental import pallas as pl
from jax.experimental.pallas import tpu as pltpu
from jax.sharding import PartitionSpec as P

EPS = 1e-6
GROUP_AXES = ('pool', 'ep')
BATCH_AXES = ('dp', 'pool', 'ep')
MESH = pl.DeviceIdType.MESH
F32 = jnp.float32
BF16 = jnp.bfloat16
VMEM_LIMIT = 66_000_000

NZ, NY = 4, 2
GROUP = 16
TOK = 128
HALF = TOK // 2
D = 896
HEADS, KV, HD, SEQ = 16, 4, 128, 32
PER_KV = HEADS // KV
TOP = 8
EXPERTS, LOCAL, FF = 256, 16, 256
SLOTS = LOCAL * TOK
BLK = 16


def rms(wide):
    return wide * lax.rsqrt(jnp.mean(wide * wide, axis=-1, keepdims=True) + EPS)


def dot(a, b):
    return jnp.dot(a, b, preferred_element_type=F32)


def split3(wide):
    high = wide.astype(BF16)
    rest = wide - high.astype(F32)
    mid = rest.astype(BF16)
    low = (rest - mid.astype(F32)).astype(BF16)
    return high, mid, low


OTHERS = [(dz, dy, dc) for dz in range(NZ) for dy in range(NY) for dc in range(2) if (dz, dy, dc) != (0, 0, 0)]


def position():
    z = lax.axis_index('pool')
    ep = lax.axis_index('ep')
    y = ep // 2
    core = lax.rem(ep, 2)

    def at(zz, dy, dc):
        return {'pool': zz, 'ep': lax.rem(y + dy, 2) * 2 + lax.rem(core + dc, 2)}
    return z, y, core, at


def slot(zz, dy, dc):
    return (zz * 2 + dy) * 2 + dc


def remote(src, dst, send, recv, target):
    return pltpu.make_async_remote_copy(src_ref=src, dst_ref=dst, send_sem=send, recv_sem=recv, device_id=target, device_id_type=MESH)


EDGE = 16
GATHER = ((0, 80), (80, 48))
REDUCE = ((0, EDGE), (EDGE, 56), (72, 56))


def kernel(layers, x_ref, kc_hbm, vc_hbm, len_ref, wq_hbm, wk_hbm, wv_hbm, wo_hbm, wr_hbm, ids_own, wg_hbm, wu_hbm, wd_hbm, out_ref,
           wg, wu, wd, wr, rows, xs, ys, pick, mix, gates, pos, jpos, tgt, base_ref, ids_ref,
           x_s, a_ref, u_ref, gate_ref, qs, ks, vs, mixed,
           core_in, y_in, y_edge, right_in, right_edge, left_in, left_edge,
           wsem, asem, ksem, vsem, isem_s, isem_r, gsem_s, gsem_r, az_s, az_r, ay_s, ay_r, ac_s, ac_r,
           rc_s, rc_r, ry_s, ry_r, rr_s, rr_r, rl_s, rl_r):
    z, y, core, at = position()
    first = (z * 4 + y * 2 + core) * LOCAL
    side = z // 2
    near = z - side * (2 * z - 3)
    mirror = lambda v: v + side * (3 - 2 * v)
    n1, n2, n3 = mirror(1 - near), mirror(2), mirror(3)
    order = (mirror(3), mirror(2), mirror(1 - near), mirror(near))
    inside, end = near == 1, near == 0

    barrier = pltpu.get_barrier_semaphore()
    for dz, dy, dc in OTHERS:
        pl.semaphore_signal(barrier, inc=1, device_id=at(lax.rem(z + dz, NZ), dy, dc), device_id_type=MESH)

    def attention_loads(layer):
        pairs = [(wq_hbm.at[layer, :, pl.ds(c * FF, FF)], wg.at[c]) for c in range(8)]
        pairs += [(wk_hbm.at[layer, :, pl.ds(c * FF, FF)], wg.at[8 + c]) for c in range(2)]
        pairs += [(wv_hbm.at[layer, :, pl.ds(c * FF, FF)], wg.at[10 + c]) for c in range(2)]
        pairs += [(wo_hbm.at[layer, pl.ds(c * FF, FF)], wd.at[c]) for c in range(8)]
        pairs += [(wr_hbm.at[layer], wr)]
        return [pltpu.make_async_copy(src, dst, asem.at[i]) for i, (src, dst) in enumerate(pairs)]

    def cache_loads(layer):
        copies = []
        for hbm, start, sem in ((kc_hbm, 0, ksem), (vc_hbm, TOK // BLK, vsem)):
            for q in range(BLK):
                copies.append(pltpu.make_async_copy(hbm.at[layer, :, q], pick.at[pl.ds(start, TOK // BLK), :, pl.ds(q * HD, HD)], sem.at[q]))
        return copies

    chunk = 4

    def expert_loads(layer):
        copies = []
        for i in range(LOCAL // chunk):
            part = pl.ds(i * chunk, chunk)
            for j, (src, dst) in enumerate(((wg_hbm, wg), (wu_hbm, wu), (wd_hbm, wd))):
                copies.append(pltpu.make_async_copy(src.at[layer, part], dst.at[part], wsem.at[j, i]))
        return copies

    def start(copies):
        for copy in copies:
            copy.start()

    def ids_copy(dz, dy, dc):
        me = slot(z, dy, dc)
        return remote(ids_own, ids_ref.at[me], isem_s.at[dz * 4 + dy * 2 + dc], isem_r.at[me], at(lax.rem(z + dz, NZ), dy, dc))

    def ids_start():
        pl.semaphore_wait(barrier, len(OTHERS))
        for o in OTHERS:
            ids_copy(*o).start()
        ids_ref[slot(z, 0, 0)] = ids_own[...]

    def ids_wait():
        for dz, dy, dc in OTHERS:
            ids_copy(dz, dy, dc).wait_send()
            i = slot(lax.rem(z + dz, NZ), dy, dc)
            remote(ids_own, ids_ref.at[i], isem_s.at[0], isem_r.at[i], at(z, 0, 1)).wait_recv()

    scale = HD ** -0.5
    pair_lane = lax.broadcasted_iota(jnp.int32, (HEADS, SEQ * KV), 1)
    pair_head = lax.broadcasted_iota(jnp.int32, (HEADS, SEQ * KV), 0)
    pair_pos = jnp.where(lax.rem(pair_lane, KV) == pair_head // PER_KV, pair_lane // KV, SEQ)

    def attend(b, carry):
        tok = b * BLK
        part = pl.ds(tok * HEADS, BLK * HEADS)
        q_wide = qs[part, :]
        q_blk = q_wide.astype(BF16)
        score_list, mask_list = [], []
        for t in range(BLK):
            keys = pick[b, :, t * HD:(t + 1) * HD]
            score_list.append(lax.dot_general(q_blk[t * HEADS:(t + 1) * HEADS], keys, (((1,), (1,)), ((), ())), preferred_element_type=F32))
            mask_list.append(pair_pos < len_ref[0, tok + t])
        score = jnp.concatenate(score_list, axis=0) * scale
        mask = jnp.concatenate(mask_list, axis=0)
        score = jnp.where(mask, score, -jnp.inf)
        score_new = jnp.sum(q_wide * ks[part, :], axis=-1, keepdims=True) * scale
        peak = jnp.maximum(jnp.max(score, axis=-1, keepdims=True), score_new)
        prob = jnp.exp(score - peak)
        prob_new = jnp.exp(score_new - peak)
        total = jnp.sum(prob, axis=-1, keepdims=True) + prob_new
        prob = (prob / total).astype(BF16)
        prob_new = (prob_new / total).astype(BF16).astype(F32)
        out = [dot(prob[t * HEADS:(t + 1) * HEADS], pick[TOK // BLK + b, :, t * HD:(t + 1) * HD]) for t in range(BLK)]
        out = jnp.concatenate(out, axis=0) + prob_new * vs[part, :]
        qs[part, :] = out.astype(BF16).astype(F32)
        return carry

    def attention(layer, x_from):
        loads = attention_loads(layer)
        x = x_from[...].astype(F32)
        h = rms(x).astype(BF16)
        with jax.named_scope('qkv'):
            for c in range(8):
                loads[c].wait()
                q = dot(h, wg[c]).astype(BF16).astype(F32)
                for j in range(2):
                    qs[pl.ds(c * 2 + j, TOK, stride=HEADS), :] = q[:, j * HD:(j + 1) * HD]
            for c in range(2):
                loads[8 + c].wait()
                loads[10 + c].wait()
                k_new = dot(h, wg[8 + c]).astype(BF16).astype(F32)
                v_new = dot(h, wg[10 + c]).astype(BF16).astype(F32)
                for i in range(8):
                    j = i // PER_KV
                    ks[pl.ds(c * 8 + i, TOK, stride=HEADS), :] = k_new[:, j * HD:(j + 1) * HD]
                    vs[pl.ds(c * 8 + i, TOK, stride=HEADS), :] = v_new[:, j * HD:(j + 1) * HD]
        if layer == 0:
            with jax.named_scope('barrier'):
                ids_start()
        with jax.named_scope('att'):
            for copy in cache_loads(layer):
                copy.wait()
            lax.fori_loop(0, TOK // BLK, attend, 0)
        with jax.named_scope('post'):
            for i in range(HEADS):
                mixed[:, i * HD:(i + 1) * HD] = qs[pl.ds(i, TOK, stride=HEADS), :].astype(BF16)
            for copy in loads[12:]:
                copy.wait()
            a = (x + dot(mixed[...], wd[0:8].reshape(HEADS * HD, D))).astype(BF16)
            a_ref[...] = a
            u = rms(a.astype(F32)).astype(BF16)
            u_ref[...] = u
            high, mid, low3 = split3(wr[...])
            logits = ((dot(u, low3) + dot(u, mid)) + dot(u, high)).T
            row = lax.broadcasted_iota(jnp.int32, (EXPERTS, TOK), 0)
            chosen = [jnp.sum(jnp.where(row == ids_own[layer, k:k + 1, :], logits, 0.0), axis=0, keepdims=True) for k in range(TOP)]
            chosen = jnp.concatenate(chosen, axis=0)
            weight = jnp.exp(chosen - jnp.max(chosen, axis=0, keepdims=True))
            gate_ref[...] = weight / jnp.sum(weight, axis=0, keepdims=True)

    expert = lax.broadcasted_iota(jnp.int32, (LOCAL, TOK), 0) + first
    tri = (lax.broadcasted_iota(jnp.int32, (TOK, TOK), 0) < lax.broadcasted_iota(jnp.int32, (TOK, TOK), 1)).astype(BF16)
    ones = jnp.ones((TOK, TOK), BF16)
    low = (lax.broadcasted_iota(jnp.int32, (LOCAL, LOCAL), 1) < lax.broadcasted_iota(jnp.int32, (LOCAL, LOCAL), 0)).astype(BF16)
    lane = lax.broadcasted_iota(jnp.int32, (LOCAL, TOK), 1).astype(F32)
    sub = lax.broadcasted_iota(jnp.int32, (TOK, TOK), 0).astype(F32)
    sub16 = sub.astype(BF16)

    def onehot(row):
        row16 = jnp.broadcast_to(row, (16, TOK)).astype(BF16)
        return jnp.where(sub16 == jnp.concatenate([row16] * (TOK // 16), axis=0), jnp.ones((TOK, TOK), BF16), jnp.zeros((TOK, TOK), BF16))

    def plan(layer, s, base):
        ids = ids_ref[s, layer]
        hit = jnp.zeros((LOCAL, TOK), F32)
        for k in range(TOP):
            hit = hit + jnp.where(expert == ids[k:k + 1, :], 1.0, 0.0)
        hit16 = hit.astype(BF16)
        rank = dot(hit16, tri)
        count = dot(hit16, ones)
        offset = dot(low, count.astype(BF16))
        pos[s] = jnp.where(hit > 0, base + rank, -1.0)
        jpos[s] = jnp.where(hit > 0, offset + rank, -1.0)
        local = lane - base
        tgt[s] = jnp.where((local >= 0) & (local < count), local + offset, -1.0)
        return base + count

    def plan_part(layer, begin, stop):
        if begin == 0:
            base_ref[...] = jnp.zeros((LOCAL, TOK), F32)
        base_ref[...] = lax.fori_loop(begin, stop, functools.partial(plan, layer), base_ref[...], unroll=2)

    def block(zz, dy, dc, start, count):
        return rows.at[zz * 2 + dy, pl.ds(dc * TOK + start, count)]

    def z_send(zz, c, step):
        if c == 2:
            src = block(zz, 1, 0, 0, EDGE)
        else:
            src = block(zz, 0, 0, *GATHER[c])
        return remote(src, src, az_s.at[zz, c, (step + 1) // 2], az_r.at[zz, c], at(z + step, 0, 0))

    def own_z_send(c, step):
        return remote(u_ref.at[pl.ds(*GATHER[c])], block(z, 0, 0, *GATHER[c]), az_s.at[z, c, (step + 1) // 2], az_r.at[z, c], at(z + step, 0, 0))

    def z_arrival(zz, c):
        src = block(zz, 1, 0, 0, EDGE) if c == 2 else block(zz, 0, 0, *GATHER[c])
        return remote(src, src, az_s.at[zz, c, 0], az_r.at[zz, c], at(z, 0, 1))

    def y_piece(c):
        start, count = GATHER[c]
        return (EDGE, count - EDGE) if c == 0 else (start, count)

    def y_send(zz, c):
        return remote(block(zz, 0, 0, *y_piece(c)), block(zz, 1, 0, *y_piece(c)), ay_s.at[zz, c], ay_r.at[zz, c], at(z, 1, 0))

    def own_y_send(c):
        return remote(u_ref.at[pl.ds(*GATHER[c])], block(z, 1, 0, *GATHER[c]), ay_s.at[z, c], ay_r.at[z, c], at(z, 1, 0))

    def core_send(zz, dy):
        return remote(block(zz, dy, 0, 0, TOK), block(zz, dy, 1, 0, TOK), ac_s.at[zz, dy], ac_r.at[zz, dy], at(z, 0, 1))

    def own_core_send():
        return remote(u_ref, block(z, 0, 1, 0, TOK), ac_s.at[z, 0], ac_r.at[z, 0], at(z, 0, 1))

    def both_ways(make, act):
        @pl.when(z < NZ - 1)
        def _():
            getattr(make(1), act)()

        @pl.when(z > 0)
        def _():
            getattr(make(-1), act)()

    def onward(zz, c, act):
        @pl.when((zz < z) & (z < NZ - 1))
        def _():
            getattr(z_send(zz, c, 1), act)()

        @pl.when((zz > z) & (z > 0))
        def _():
            getattr(z_send(zz, c, -1), act)()

    def gate_copy(dz, dy, dc):
        me = slot(z, dy, dc)
        return remote(gate_ref, gates.at[me], gsem_s.at[dz * 4 + dy * 2 + dc], gsem_r.at[me], at(lax.rem(z + dz, NZ), dy, dc))

    per = 4

    def fill(zz, dy, fresh=False):
        chip = zz * 2 + dy

        def body(i, carry):
            picks = []
            for j in range(per):
                e = i * per + j
                picks.append(jnp.concatenate([onehot(pos[chip * 2 + dc, pl.ds(e, 1), :]) for dc in range(2)], axis=1))
            got = dot(jnp.concatenate(picks, axis=0), rows[chip])
            where = pl.ds(pl.multiple_of(i * per * TOK, per * TOK), per * TOK)
            if fresh:
                xs[where, :] = got
            else:
                xs[where, :] += got
            return carry
        with jax.named_scope('fill'):
            core_send(zz, dy).wait_recv()
            lax.fori_loop(0, LOCAL // per, body, 0)

    def arrive(zz, c):
        z_arrival(zz, c).wait_recv()
        onward(zz, c, 'start')
        if c < 2:
            y_send(zz, c).start()
        if c == 1:
            core_send(zz, 0).start()

    def arrive_y(zz):
        for c in range(2):
            y_send(zz, c).wait_recv()
        core_send(zz, 1).start()

    def gather(layer):
        own_core_send().start()
        for c in range(2):
            both_ways(lambda step: own_z_send(c, step), 'start')
            own_y_send(c).start()

        for o in OTHERS:
            gate_copy(*o).start()
        gates[slot(z, 0, 0)] = gate_ref[...]
        rows[z * 2, pl.ds(0, TOK), :] = u_ref[...]

        start(expert_loads(layer))
        if layer == 0:
            with jax.named_scope('plan'):
                ids_wait()
                plan_part(0, 0, GROUP)
        fill(z, 0, True)
        arrive(n1, 0)
        pl.when(inside)(lambda: arrive(n2, 0))
        own_y_send(0).wait_recv()
        both_ways(lambda step: z_send(z, 2, step), 'start')
        arrive(n1, 1)
        pl.when(inside)(lambda: arrive(n2, 1))
        own_y_send(1).wait_recv()
        core_send(z, 1).start()
        fill(n1, 0)
        pl.when(end)(lambda: arrive(n2, 0))
        pl.when(inside)(lambda: arrive(n3, 0))
        arrive(n1, 2)
        pl.when(inside)(lambda: arrive(n2, 2))
        fill(z, 1)
        pl.when(end)(lambda: arrive(n2, 1))
        pl.when(inside)(lambda: arrive(n3, 1))
        fill(n2, 0)
        pl.when(end)(lambda: arrive(n2, 2))
        pl.when(end)(lambda: arrive(n3, 0))
        arrive_y(n1)
        fill(n1, 1)
        pl.when(end)(lambda: arrive(n3, 1))
        arrive_y(n2)
        fill(n3, 0)
        arrive(n3, 2)
        fill(n2, 1)
        arrive_y(n3)
        fill(n3, 1)

        own_core_send().wait_send()
        for c in range(2):
            own_y_send(c).wait_send()
            both_ways(lambda step: own_z_send(c, step), 'wait_send')
        both_ways(lambda step: z_send(z, 2, step), 'wait_send')
        for zz in (n1, n2, n3):
            core_send(zz, 0).wait_send()
            for c in range(3):
                onward(zz, c, 'wait_send')
                if c < 2:
                    y_send(zz, c).wait_send()
        for zz in range(NZ):
            core_send(zz, 1).wait_send()
        for dz, dy, dc in OTHERS:
            gate_copy(dz, dy, dc).wait_send()
            s = slot(lax.rem(z + dz, NZ), dy, dc)
            remote(gate_ref, gates.at[s], gsem_s.at[0], gsem_r.at[s], at(z, 0, 1)).wait_recv()

    def ready(layer, s):
        ids = ids_ref[s, layer]
        gate = gates[s]
        g = jnp.zeros((LOCAL, TOK), F32)
        for k in range(TOP):
            g = g + jnp.where(expert == ids[k:k + 1, :], gate[k:k + 1, :], 0.0)
        jp = jpos[s]
        acc = jnp.zeros((TOK, TOK), F32)
        for e in range(LOCAL):
            acc = acc + jnp.where(sub == jp[e:e + 1, :], g[e:e + 1, :], 0.0)
        for i, part in enumerate(split3(acc.T)):
            mix[s, i * TOK:(i + 1) * TOK, :] = part
        for e in range(LOCAL):
            pick[s, :, e * TOK:(e + 1) * TOK] = onehot(tgt[s, e:e + 1, :])

    def experts(layer, e, carry):
        ready(layer, e)
        window = pl.ds(pl.multiple_of(e * TOK, TOK), TOK)
        x = xs[window, :].astype(BF16)
        inner = (jax.nn.silu(dot(x, wg[e])) * dot(x, wu[e])).astype(BF16)
        ys[window, :] = dot(inner, wd[e]).astype(BF16)
        return carry
    def all_experts(layer):
        with jax.named_scope('experts'):
            weights = expert_loads(layer)
            for i in range(LOCAL // chunk):
                for copy in weights[3 * i:3 * i + 3]:
                    copy.wait()
                lax.fori_loop(i * chunk, (i + 1) * chunk, functools.partial(experts, layer), 0)

    def own_part(i, start=0, count=TOK):
        return xs.at[pl.ds(pl.multiple_of(i * TOK + start, 8), count)]

    def far_part(i):
        return xs.at[pl.ds(pl.multiple_of((NZ * NY + i) * TOK, TOK), TOK)]

    def core_copy(i):
        return remote(far_part(i), core_in.at[i], rc_s.at[i], rc_r.at[i], at(z, 0, 1))

    def y_copy(zd, c):
        part = pl.ds(*REDUCE[c])
        if c == 0:
            dst = y_edge
        else:
            dst = y_in.at[zd, part]
        return remote(own_part(zd * 2 + 1, *REDUCE[c]), dst, ry_s.at[zd, c], ry_r.at[zd, c], at(z, 1, 0))

    def z_copy(zd, c, step, target=None):
        main, edge, send, recv = (right_in, right_edge, rr_s, rr_r) if step == 1 else (left_in, left_edge, rl_s, rl_r)
        target = at(z + step, 0, 0) if target is None else target
        if c == 3:
            return remote(own_part(zd * 2 + 1, 0, EDGE), edge.at[zd], send.at[zd, c], recv.at[zd, c], target)
        return remote(own_part(zd * 2, *REDUCE[c]), main.at[zd, pl.ds(*REDUCE[c])], send.at[zd, c], recv.at[zd, c], target)

    def take(zd, c, step):
        z_copy(zd, c, step, at(z, 0, 1)).wait_recv()
        main, edge = (right_in, right_edge) if step == 1 else (left_in, left_edge)
        if c == 3:
            own_part(zd * 2 + 1, 0, EDGE)[...] += edge[zd]
        else:
            own_part(zd * 2, *REDUCE[c])[...] += main[zd, pl.ds(*REDUCE[c])]

    def chain(zd, c):
        @pl.when(zd > z)
        def _():
            @pl.when(z > 0)
            def _():
                take(zd, c, 1)
            z_copy(zd, c, 1).start()

        @pl.when(zd < z)
        def _():
            @pl.when(z < NZ - 1)
            def _():
                take(zd, c, -1)
            z_copy(zd, c, -1).start()

    def last(c):
        @pl.when(z > 0)
        def _():
            take(z, c, 1)

        @pl.when(z < NZ - 1)
        def _():
            take(z, c, -1)

    def cross(zd, c):
        y_copy(zd, c).wait_recv()
        own_part(zd * 2, *REDUCE[c])[...] += y_in[zd, pl.ds(*REDUCE[c])]

    def edges(zd):
        chain(zd, 0)
        chain(zd, 3)

    def piece(zd, c):
        cross(zd, c)
        chain(zd, c)

    targets = [order[i] * 2 + dy for i in range(NZ) for dy in (1, 0)]

    def pick_target(j):
        value = targets[0]
        for i in range(1, len(targets)):
            value = jnp.where(j == i, targets[i], value)
        return value

    def finish(j):
        i = pick_target(j)
        core_copy(i).wait_recv()
        own_part(i)[...] += core_in[i]

        @pl.when(lax.rem(i, 2) == 1)
        def _():
            for c in (1, 2):
                y_copy(i // 2, c).start()

    def combine(j, carry):
        i = pick_target(j)
        s = i * 2
        pairs = dot(pick[pl.ds(s, 2)].reshape(2 * TOK, SLOTS), ys[...]).astype(BF16)
        for dc, part in ((1, far_part), (0, own_part)):
            got = dot(mix[s + dc], pairs[dc * TOK:(dc + 1) * TOK])
            part(i)[...] = (got[2 * TOK:] + got[TOK:2 * TOK]) + got[:TOK]
            if dc == 1:
                core_copy(i).start()

        @pl.when(j > 0)
        def _():
            finish(j - 1)

        @pl.when(end & (j == 2))
        def _():
            edges(order[0])

        @pl.when(end & (j == 4))
        def _():
            edges(order[1])

        @pl.when(end & (j == 5))
        def _():
            piece(order[0], 1)

        @pl.when(end & (j == 7))
        def _():
            piece(order[0], 2)

        @pl.when(inside & (j == 5))
        def _():
            edges(order[0])

        @pl.when(inside & (j == 7))
        def _():
            edges(order[1])
        return carry

    def reduce(layer):
        def ahead(i):
            if layer + 1 < layers:
                plan_part(layer + 1, i * 4, i * 4 + 4)

        with jax.named_scope('combine'):
            lax.fori_loop(0, len(targets), combine, 0)
        if layer + 1 < layers:
            start(cache_loads(layer + 1))

        with jax.named_scope('chain'):
            finish(len(targets) - 1)

            edges(order[2])

            @pl.when(inside)
            def _():
                piece(order[0], 1)
            ahead(0)

            @pl.when(inside)
            def _():
                piece(order[0], 2)
            ahead(1)
            piece(order[1], 1)
            ahead(2)
            piece(order[1], 2)
            last(3)
            y_copy(z, 0).start()
            ahead(3)
            piece(order[2], 1)
            piece(order[2], 2)
            last(0)
            for c in (1, 2):
                cross(z, c)
                last(c)
            y_copy(z, 0).wait_recv()
            own_part(z * 2, 0, EDGE)[...] += y_edge[...]
            dest = x_s if layer + 1 < layers else out_ref
            dest[...] = (a_ref[...].astype(F32) + own_part(z * 2)[...]).astype(BF16)

        for zz in range(NZ):
            for dy in range(2):
                core_copy(zz * 2 + dy).wait_send()
            for c in (1, 2):
                y_copy(zz, c).wait_send()
            for c in range(4):
                @pl.when(zz > z)
                def _():
                    z_copy(zz, c, 1).wait_send()

                @pl.when(zz < z)
                def _():
                    z_copy(zz, c, -1).wait_send()
        y_copy(z, 0).wait_send()


    start(attention_loads(0))
    start(cache_loads(0))
    for layer in range(layers):
        attention(layer, x_ref if layer == 0 else x_s)
        gather(layer)
        all_experts(layer)
        if layer + 1 < layers:
            start(attention_loads(layer + 1))
        reduce(layer)


def solution(mesh):
    def device_step(hidden, k_cache, v_cache, lengths, w_query, w_key, w_value, w_out, w_router, expert_ids, w_gate, w_up, w_down):
        layers = expert_ids.shape[0]
        kc = k_cache.reshape(layers, TOK // BLK, BLK, SEQ * KV, HD)
        vc = v_cache.reshape(layers, TOK // BLK, BLK, SEQ * KV, HD)
        ids = jnp.swapaxes(expert_ids, 1, 2)
        vmem = pl.BlockSpec(memory_space=pltpu.VMEM)
        hbm = pl.BlockSpec(memory_space=pl.ANY)
        sem = pltpu.SemaphoreType.DMA
        buf = pltpu.VMEM
        return pl.pallas_call(
            functools.partial(kernel, layers),
            out_shape=jax.ShapeDtypeStruct((TOK, D), BF16),
            in_specs=[vmem, hbm, hbm, pl.BlockSpec(memory_space=pltpu.SMEM), hbm, hbm, hbm, hbm, hbm, vmem, hbm, hbm, hbm],
            out_specs=vmem,
            scratch_shapes=[
                buf((LOCAL, D, FF), BF16), buf((LOCAL, D, FF), BF16), buf((LOCAL, FF, D), BF16), buf((D, EXPERTS), F32),
                buf((NZ * NY, 2 * TOK, D), BF16), buf((SLOTS, D), F32), buf((SLOTS, D), BF16), buf((GROUP, TOK, SLOTS), BF16), buf((GROUP, 3 * TOK, TOK), BF16),
                buf((GROUP, TOP, TOK), F32), buf((GROUP, LOCAL, TOK), F32), buf((GROUP, LOCAL, TOK), F32), buf((GROUP, LOCAL, TOK), F32),
                buf((LOCAL, TOK), F32), buf((GROUP,) + ids.shape, jnp.int32),
                buf((TOK, D), BF16), buf((TOK, D), BF16), buf((TOK, D), BF16), buf((TOP, TOK), F32),
                buf((TOK * HEADS, HD), F32), buf((TOK * HEADS, HD), F32), buf((TOK * HEADS, HD), F32), buf((TOK, HEADS * HD), BF16),
                buf((NZ * NY, TOK, D), F32), buf((NZ, TOK, D), F32), buf((EDGE, D), F32),
                buf((NZ, TOK, D), F32), buf((NZ, EDGE, D), F32), buf((NZ, TOK, D), F32), buf((NZ, EDGE, D), F32),
                sem((3, 4)), sem((21,)), sem((BLK,)), sem((BLK,)), sem((GROUP,)), sem((GROUP,)), sem((GROUP,)), sem((GROUP,)),
                sem((NZ, 3, 2)), sem((NZ, 3)), sem((NZ, 2)), sem((NZ, 2)), sem((NZ, 2)), sem((NZ, 2)),
                sem((NZ * NY,)), sem((NZ * NY,)), sem((NZ, 3)), sem((NZ, 3)), sem((NZ, 4)), sem((NZ, 4)), sem((NZ, 4)), sem((NZ, 4)),
            ],
            compiler_params=pltpu.CompilerParams(vmem_limit_bytes=67_043_328, collective_id=0, has_side_effects=True),
            name='layers',
        )(hidden, kc, vc, lengths[None], w_query, w_key, w_value, w_out, w_router, ids, w_gate, w_up, w_down)

    cache_spec = P(None, BATCH_AXES, None, None, None)
    expert_spec = P(None, GROUP_AXES, None, None)
    in_specs = (P(BATCH_AXES, None), cache_spec, cache_spec, P(BATCH_AXES), P(), P(), P(), P(), P(), P(None, BATCH_AXES, None), expert_spec, expert_spec, expert_spec)
    return jax.shard_map(device_step, mesh=mesh, in_specs=in_specs, out_specs=P(BATCH_AXES, None), check_vma=False)
```

time: 217 us -> 200 us (0.922)
  Pallas kernels: 215 us -> 198 us
    pallas_call x4 -> x1, Pallas kernels: 215 us -> 198 us  [device_step(): pl.pallas_call(functools.partial(kernel, layers), out_shape=jax.ShapeDtyp...]
where the time goes in v3:
time: 200 us; the launch traced here: 199 us
  Pallas kernels  198 us (99%)
    pallas_call x1, Pallas kernels, device_step(): pl.pallas_call(functools.partial(kernel, layers), out_shape=jax.ShapeDtyp...  198 us

profile of v3, /device:TPU:0, one launch (start us, length us, event | category | flops | bytes accessed | tf_op | source)
XLA Modules:
  0.0 199.4 jit_solution(12126050796800124723)
XLA Ops:
  0.0 197.7 %layers.1 = bf16[128,896]{1,0:T(8,128)(2,1)} custom-call(bf16[128,896]{1,0:T(8,128)(2,1)} %x_ref.1, bf16[2,8,16,128,128]{4,3,2,1,0:T(8,128)(2,1)} %bitcast.4, bf16[2,8,16,128,128]{4,3,2,1,0:T(8,128)(2,1)} %bitcast.5, s32[1,128]{1,0:T(1,128)} %bitcast.7, bf16[2,896,2048]{2,1,0:T(8,128)(2,1)} %wq_hbm.1, bf16[2,896,512]{2,1,0:T(8,128)(2,1)} %wk_hbm.1, ...), custom_call_target="tpu_custom_call" | custom-call | tf_op jit(solution)/shard_map/layers/pallas_call | solution.py:629
  197.7 1.6 copy.15

commit v4 on v3

--- a/solution.py
+++ b/solution.py
@@ -67,8 +67,11 @@
 
 
 EDGE = 16
-GATHER = ((0, 80), (80, 48))
-REDUCE = ((0, EDGE), (EDGE, 56), (72, 56))
+PARTS = ((0, 64), (64, 64))
+GATHER = PARTS
+HALVES = ((0, EDGE), (EDGE, 48), PARTS[1])
+EVEN = ((0, EDGE), (EDGE, 56), (72, 56))
+WHOLE = (0, TOK)
 
 
 def kernel(layers, x_ref, kc_hbm, vc_hbm, len_ref, wq_hbm, wk_hbm, wv_hbm, wo_hbm, wr_hbm, ids_own, wg_hbm, wu_hbm, wd_hbm, out_ref,
@@ -86,6 +89,9 @@
     order = (mirror(3), mirror(2), mirror(1 - near), mirror(near))
     inside, end = near == 1, near == 0
 
+    mine = slot(z, 0, 0)
+    partner, across = at(z, 0, 1), at(z, 1, 0)
+    along = lambda zz: at(zz, 0, 0)
     barrier = pltpu.get_barrier_semaphore()
     for dz, dy, dc in OTHERS:
         pl.semaphore_signal(barrier, inc=1, device_id=at(lax.rem(z + dz, NZ), dy, dc), device_id_type=MESH)
@@ -127,13 +133,13 @@
         pl.semaphore_wait(barrier, len(OTHERS))
         for o in OTHERS:
             ids_copy(*o).start()
-        ids_ref[slot(z, 0, 0)] = ids_own[...]
+        ids_ref[mine] = ids_own[...]
 
     def ids_wait():
         for dz, dy, dc in OTHERS:
             ids_copy(dz, dy, dc).wait_send()
             i = slot(lax.rem(z + dz, NZ), dy, dc)
-            remote(ids_own, ids_ref.at[i], isem_s.at[0], isem_r.at[i], at(z, 0, 1)).wait_recv()
+            remote(ids_own, ids_ref.at[i], isem_s.at[0], isem_r.at[i], partner).wait_recv()
 
     scale = HD ** -0.5
     pair_lane = lax.broadcasted_iota(jnp.int32, (HEADS, SEQ * KV), 1)
@@ -165,41 +171,52 @@
         qs[part, :] = out.astype(BF16).astype(F32)
         return carry
 
-    def attention(layer, x_from):
+    def project(layer, span, x_from):
         loads = attention_loads(layer)
-        x = x_from[...].astype(F32)
-        h = rms(x).astype(BF16)
+        begin, count = span
         with jax.named_scope('qkv'):
+            h = rms(x_from[begin:begin + count].astype(F32)).astype(BF16)
+
+            def spread(ref, head, block):
+                ref[pl.ds(begin * HEADS + head, count, stride=HEADS), :] = block
+
             for c in range(8):
-                loads[c].wait()
+                if begin == 0:
+                    loads[c].wait()
                 q = dot(h, wg[c]).astype(BF16).astype(F32)
                 for j in range(2):
-                    qs[pl.ds(c * 2 + j, TOK, stride=HEADS), :] = q[:, j * HD:(j + 1) * HD]
+                    spread(qs, c * 2 + j, q[:, j * HD:(j + 1) * HD])
             for c in range(2):
-                loads[8 + c].wait()
-                loads[10 + c].wait()
+                if begin == 0:
+                    loads[8 + c].wait()
+                    loads[10 + c].wait()
                 k_new = dot(h, wg[8 + c]).astype(BF16).astype(F32)
                 v_new = dot(h, wg[10 + c]).astype(BF16).astype(F32)
                 for i in range(8):
                     j = i // PER_KV
-                    ks[pl.ds(c * 8 + i, TOK, stride=HEADS), :] = k_new[:, j * HD:(j + 1) * HD]
-                    vs[pl.ds(c * 8 + i, TOK, stride=HEADS), :] = v_new[:, j * HD:(j + 1) * HD]
-        if layer == 0:
-            with jax.named_scope('barrier'):
-                ids_start()
+                    spread(ks, c * 8 + i, k_new[:, j * HD:(j + 1) * HD])
+                    spread(vs, c * 8 + i, v_new[:, j * HD:(j + 1) * HD])
+
+    def attend_blocks(first_block, stop):
         with jax.named_scope('att'):
-            for copy in cache_loads(layer):
-                copy.wait()
-            lax.fori_loop(0, TOK // BLK, attend, 0)
+            lax.fori_loop(first_block, stop, attend, 0, unroll=2)
+
+    def project_out(layer, span, x_from):
+        begin, count = span
         with jax.named_scope('post'):
             for i in range(HEADS):
-                mixed[:, i * HD:(i + 1) * HD] = qs[pl.ds(i, TOK, stride=HEADS), :].astype(BF16)
-            for copy in loads[12:]:
-                copy.wait()
-            a = (x + dot(mixed[...], wd[0:8].reshape(HEADS * HD, D))).astype(BF16)
-            a_ref[...] = a
-            u = rms(a.astype(F32)).astype(BF16)
-            u_ref[...] = u
+                mixed[:count, i * HD:(i + 1) * HD] = qs[pl.ds(begin * HEADS + i, count, stride=HEADS), :].astype(BF16)
+            if begin == 0:
+                for copy in attention_loads(layer)[12:]:
+                    copy.wait()
+            x = x_from[begin:begin + count].astype(F32)
+            a = (x + dot(mixed[:count, :], wd[0:8].reshape(HEADS * HD, D))).astype(BF16)
+            a_ref[begin:begin + count] = a
+            u_ref[begin:begin + count] = rms(a.astype(F32)).astype(BF16)
+
+    def route(layer):
+        with jax.named_scope('route'):
+            u = u_ref[...]
             high, mid, low3 = split3(wr[...])
             logits = ((dot(u, low3) + dot(u, mid)) + dot(u, high)).T
             row = lax.broadcasted_iota(jnp.int32, (EXPERTS, TOK), 0)
@@ -207,6 +224,25 @@
             chosen = jnp.concatenate(chosen, axis=0)
             weight = jnp.exp(chosen - jnp.max(chosen, axis=0, keepdims=True))
             gate_ref[...] = weight / jnp.sum(weight, axis=0, keepdims=True)
+
+    def send_part(part):
+        both_ways(lambda step: own_z_send(part, step), 'start')
+        own_y_send(part).start()
+
+    def first_part(layer, span, x_from, between):
+        project(layer, span, x_from)
+        between(0)
+        for copy in cache_loads(layer):
+            copy.wait()
+        if layer == 0:
+            attend_blocks(0, 2)
+            with jax.named_scope('barrier'):
+                ids_start()
+            attend_blocks(2, span[1] // BLK)
+        else:
+            attend_blocks(0, span[1] // BLK)
+        between(1)
+        project_out(layer, span, x_from)
 
     expert = lax.broadcasted_iota(jnp.int32, (LOCAL, TOK), 0) + first
     tri = (lax.broadcasted_iota(jnp.int32, (TOK, TOK), 0) < lax.broadcasted_iota(jnp.int32, (TOK, TOK), 1)).astype(BF16)
@@ -248,30 +284,30 @@
             src = block(zz, 1, 0, 0, EDGE)
         else:
             src = block(zz, 0, 0, *GATHER[c])
-        return remote(src, src, az_s.at[zz, c, (step + 1) // 2], az_r.at[zz, c], at(z + step, 0, 0))
+        return remote(src, src, az_s.at[zz, c, (step + 1) // 2], az_r.at[zz, c], along(z + step))
 
     def own_z_send(c, step):
-        return remote(u_ref.at[pl.ds(*GATHER[c])], block(z, 0, 0, *GATHER[c]), az_s.at[z, c, (step + 1) // 2], az_r.at[z, c], at(z + step, 0, 0))
+        return remote(u_ref.at[pl.ds(*GATHER[c])], block(z, 0, 0, *GATHER[c]), az_s.at[z, c, (step + 1) // 2], az_r.at[z, c], along(z + step))
 
     def z_arrival(zz, c):
         src = block(zz, 1, 0, 0, EDGE) if c == 2 else block(zz, 0, 0, *GATHER[c])
-        return remote(src, src, az_s.at[zz, c, 0], az_r.at[zz, c], at(z, 0, 1))
+        return remote(src, src, az_s.at[zz, c, 0], az_r.at[zz, c], partner)
 
     def y_piece(c):
         start, count = GATHER[c]
         return (EDGE, count - EDGE) if c == 0 else (start, count)
 
     def y_send(zz, c):
-        return remote(block(zz, 0, 0, *y_piece(c)), block(zz, 1, 0, *y_piece(c)), ay_s.at[zz, c], ay_r.at[zz, c], at(z, 1, 0))
+        return remote(block(zz, 0, 0, *y_piece(c)), block(zz, 1, 0, *y_piece(c)), ay_s.at[zz, c], ay_r.at[zz, c], across)
 
     def own_y_send(c):
-        return remote(u_ref.at[pl.ds(*GATHER[c])], block(z, 1, 0, *GATHER[c]), ay_s.at[z, c], ay_r.at[z, c], at(z, 1, 0))
+        return remote(u_ref.at[pl.ds(*GATHER[c])], block(z, 1, 0, *GATHER[c]), ay_s.at[z, c], ay_r.at[z, c], across)
 
     def core_send(zz, dy):
-        return remote(block(zz, dy, 0, 0, TOK), block(zz, dy, 1, 0, TOK), ac_s.at[zz, dy], ac_r.at[zz, dy], at(z, 0, 1))
+        return remote(block(zz, dy, 0, 0, TOK), block(zz, dy, 1, 0, TOK), ac_s.at[zz, dy], ac_r.at[zz, dy], partner)
 
     def own_core_send():
-        return remote(u_ref, block(z, 0, 1, 0, TOK), ac_s.at[z, 0], ac_r.at[z, 0], at(z, 0, 1))
+        return remote(u_ref, block(z, 0, 1, 0, TOK), ac_s.at[z, 0], ac_r.at[z, 0], partner)
 
     def both_ways(make, act):
         @pl.when(z < NZ - 1)
@@ -329,42 +365,74 @@
             y_send(zz, c).wait_recv()
         core_send(zz, 1).start()
 
-    def gather(layer):
+    def pick_rows(s, carry):
+        for e in range(LOCAL):
+            pick[s, :, e * TOK:(e + 1) * TOK] = onehot(tgt[s, e:e + 1, :])
+        return carry
+
+    def gather(layer, x_from):
+        cut_in_two = layer > 0
+
+        def begin_first():
+            arrive(n1, 0)
+            pl.when(inside)(lambda: arrive(n2, 0))
+            own_y_send(0).wait_recv()
+            both_ways(lambda step: z_send(z, 2, step), 'start')
+
+        def edge_first():
+            arrive(n1, 2)
+            pl.when(inside)(lambda: arrive(n2, 2))
+
+        if cut_in_two:
+            middle = (PARTS[1][0] + PARTS[1][1] // 2 + BLK - 1) // BLK
+            project(layer, PARTS[1], x_from)
+            attend_blocks(PARTS[1][0] // BLK, middle)
+            begin_first()
+            attend_blocks(middle, TOK // BLK)
+            project_out(layer, PARTS[1], x_from)
+            send_part(1)
         own_core_send().start()
-        for c in range(2):
-            both_ways(lambda step: own_z_send(c, step), 'start')
-            own_y_send(c).start()
-
+        start(expert_loads(layer))
+        if cut_in_two:
+            pl.when(end)(lambda: arrive(n2, 0))
+            pl.when(inside)(lambda: arrive(n3, 0))
+        route(layer)
         for o in OTHERS:
             gate_copy(*o).start()
-        gates[slot(z, 0, 0)] = gate_ref[...]
+        gates[mine] = gate_ref[...]
         rows[z * 2, pl.ds(0, TOK), :] = u_ref[...]
-
-        start(expert_loads(layer))
         if layer == 0:
             with jax.named_scope('plan'):
                 ids_wait()
                 plan_part(0, 0, GROUP)
+        if cut_in_two:
+            edge_first()
+        if not cut_in_two:
+            begin_first()
         fill(z, 0, True)
-        arrive(n1, 0)
-        pl.when(inside)(lambda: arrive(n2, 0))
-        own_y_send(0).wait_recv()
-        both_ways(lambda step: z_send(z, 2, step), 'start')
         arrive(n1, 1)
         pl.when(inside)(lambda: arrive(n2, 1))
         own_y_send(1).wait_recv()
         core_send(z, 1).start()
+        if cut_in_two:
+            pl.when(end)(lambda: arrive(n3, 0))
+            pl.when(end)(lambda: arrive(n2, 2))
+        with jax.named_scope('picks'):
+            lax.fori_loop(0, GROUP // 2, pick_rows, 0)
         fill(n1, 0)
-        pl.when(end)(lambda: arrive(n2, 0))
-        pl.when(inside)(lambda: arrive(n3, 0))
-        arrive(n1, 2)
-        pl.when(inside)(lambda: arrive(n2, 2))
-        fill(z, 1)
+        if not cut_in_two:
+            pl.when(end)(lambda: arrive(n2, 0))
+            pl.when(inside)(lambda: arrive(n3, 0))
+            edge_first()
         pl.when(end)(lambda: arrive(n2, 1))
         pl.when(inside)(lambda: arrive(n3, 1))
+        fill(z, 1)
+        with jax.named_scope('picks'):
+            lax.fori_loop(GROUP // 2, GROUP, pick_rows, 0)
         fill(n2, 0)
-        pl.when(end)(lambda: arrive(n2, 2))
-        pl.when(end)(lambda: arrive(n3, 0))
+        if not cut_in_two:
+            pl.when(end)(lambda: arrive(n2, 2))
+            pl.when(end)(lambda: arrive(n3, 0))
         arrive_y(n1)
         fill(n1, 1)
         pl.when(end)(lambda: arrive(n3, 1))
@@ -391,7 +459,7 @@
         for dz, dy, dc in OTHERS:
             gate_copy(dz, dy, dc).wait_send()
             s = slot(lax.rem(z + dz, NZ), dy, dc)
-            remote(gate_ref, gates.at[s], gsem_s.at[0], gsem_r.at[s], at(z, 0, 1)).wait_recv()
+            remote(gate_ref, gates.at[s], gsem_s.at[0], gsem_r.at[s], partner).wait_recv()
 
     def ready(layer, s):
         ids = ids_ref[s, layer]
@@ -405,9 +473,6 @@
             acc = acc + jnp.where(sub == jp[e:e + 1, :], g[e:e + 1, :], 0.0)
         for i, part in enumerate(split3(acc.T)):
             mix[s, i * TOK:(i + 1) * TOK, :] = part
-        for e in range(LOCAL):
-            pick[s, :, e * TOK:(e + 1) * TOK] = onehot(tgt[s, e:e + 1, :])
-
     def experts(layer, e, carry):
         ready(layer, e)
         window = pl.ds(pl.multiple_of(e * TOK, TOK), TOK)
@@ -423,6 +488,8 @@
                     copy.wait()
                 lax.fori_loop(i * chunk, (i + 1) * chunk, functools.partial(experts, layer), 0)
 
+    cut = list(HALVES)
+
     def own_part(i, start=0, count=TOK):
         return xs.at[pl.ds(pl.multiple_of(i * TOK + start, 8), count)]
 
@@ -430,30 +497,30 @@
         return xs.at[pl.ds(pl.multiple_of((NZ * NY + i) * TOK, TOK), TOK)]
 
     def core_copy(i):
-        return remote(far_part(i), core_in.at[i], rc_s.at[i], rc_r.at[i], at(z, 0, 1))
+        return remote(far_part(i), core_in.at[i], rc_s.at[i], rc_r.at[i], partner)
 
     def y_copy(zd, c):
-        part = pl.ds(*REDUCE[c])
+        part = pl.ds(*cut[c])
         if c == 0:
             dst = y_edge
         else:
             dst = y_in.at[zd, part]
-        return remote(own_part(zd * 2 + 1, *REDUCE[c]), dst, ry_s.at[zd, c], ry_r.at[zd, c], at(z, 1, 0))
+        return remote(own_part(zd * 2 + 1, *cut[c]), dst, ry_s.at[zd, c], ry_r.at[zd, c], across)
 
     def z_copy(zd, c, step, target=None):
         main, edge, send, recv = (right_in, right_edge, rr_s, rr_r) if step == 1 else (left_in, left_edge, rl_s, rl_r)
-        target = at(z + step, 0, 0) if target is None else target
+        target = along(z + step) if target is None else target
         if c == 3:
             return remote(own_part(zd * 2 + 1, 0, EDGE), edge.at[zd], send.at[zd, c], recv.at[zd, c], target)
-        return remote(own_part(zd * 2, *REDUCE[c]), main.at[zd, pl.ds(*REDUCE[c])], send.at[zd, c], recv.at[zd, c], target)
+        return remote(own_part(zd * 2, *cut[c]), main.at[zd, pl.ds(*cut[c])], send.at[zd, c], recv.at[zd, c], target)
 
     def take(zd, c, step):
-        z_copy(zd, c, step, at(z, 0, 1)).wait_recv()
+        z_copy(zd, c, step, partner).wait_recv()
         main, edge = (right_in, right_edge) if step == 1 else (left_in, left_edge)
         if c == 3:
             own_part(zd * 2 + 1, 0, EDGE)[...] += edge[zd]
         else:
-            own_part(zd * 2, *REDUCE[c])[...] += main[zd, pl.ds(*REDUCE[c])]
+            own_part(zd * 2, *cut[c])[...] += main[zd, pl.ds(*cut[c])]
 
     def chain(zd, c):
         @pl.when(zd > z)
@@ -479,9 +546,17 @@
         def _():
             take(z, c, -1)
 
+    def edge_out():
+        last(3)
+        y_copy(z, 0).start()
+
+    def edge_in():
+        y_copy(z, 0).wait_recv()
+        own_part(z * 2, 0, EDGE)[...] += y_edge[...]
+
     def cross(zd, c):
         y_copy(zd, c).wait_recv()
-        own_part(zd * 2, *REDUCE[c])[...] += y_in[zd, pl.ds(*REDUCE[c])]
+        own_part(zd * 2, *cut[c])[...] += y_in[zd, pl.ds(*cut[c])]
 
     def edges(zd):
         chain(zd, 0)
@@ -499,17 +574,18 @@
             value = jnp.where(j == i, targets[i], value)
         return value
 
-    def finish(j):
+    def finish(more, j):
         i = pick_target(j)
         core_copy(i).wait_recv()
         own_part(i)[...] += core_in[i]
 
         @pl.when(lax.rem(i, 2) == 1)
         def _():
-            for c in (1, 2):
-                y_copy(i // 2, c).start()
-
-    def combine(j, carry):
+            y_copy(i // 2, 1).start()
+            if not more:
+                y_copy(i // 2, 2).start()
+
+    def combine(more, j, carry):
         i = pick_target(j)
         s = i * 2
         pairs = dot(pick[pl.ds(s, 2)].reshape(2 * TOK, SLOTS), ys[...]).astype(BF16)
@@ -521,7 +597,7 @@
 
         @pl.when(j > 0)
         def _():
-            finish(j - 1)
+            finish(more, j - 1)
 
         @pl.when(end & (j == 2))
         def _():
@@ -537,7 +613,10 @@
 
         @pl.when(end & (j == 7))
         def _():
-            piece(order[0], 2)
+            if more:
+                piece(order[1], 1)
+            else:
+                piece(order[0], 2)
 
         @pl.when(inside & (j == 5))
         def _():
@@ -549,18 +628,28 @@
         return carry
 
     def reduce(layer):
+        more = layer + 1 < layers
+        cut[:] = HALVES if more else EVEN
+
         def ahead(i):
             if layer + 1 < layers:
                 plan_part(layer + 1, i * 4, i * 4 + 4)
 
         with jax.named_scope('combine'):
-            lax.fori_loop(0, len(targets), combine, 0)
+            lax.fori_loop(0, len(targets), functools.partial(combine, more), 0)
         if layer + 1 < layers:
             start(cache_loads(layer + 1))
 
+        dest = x_s if layer + 1 < layers else out_ref
+
+        def done(span):
+            begin, count = span
+            dest[begin:begin + count] = (a_ref[begin:begin + count].astype(F32) + own_part(z * 2, begin, count)[...]).astype(BF16)
+
         with jax.named_scope('chain'):
-            finish(len(targets) - 1)
-
+            finish(more, len(targets) - 1)
+            if more:
+                y_copy(order[0], 2).start()
             edges(order[2])
 
             @pl.when(inside)
@@ -568,26 +657,64 @@
                 piece(order[0], 1)
             ahead(0)
 
+            if more:
+                @pl.when(inside)
+                def _():
+                    piece(order[1], 1)
+                ahead(1)
+                edge_out()
+                for i in range(1, NZ):
+                    y_copy(order[i], 2).start()
+                piece(order[2], 1)
+                ahead(2)
+                last(0)
+                ahead(3)
+                cross(z, 1)
+
+                @pl.when(end)
+                def _():
+                    piece(order[0], 2)
+                last(1)
+                edge_in()
+                done(PARTS[0])
+
+            else:
+                @pl.when(inside)
+                def _():
+                    piece(order[0], 2)
+                piece(order[1], 1)
+                piece(order[1], 2)
+                edge_out()
+                piece(order[2], 1)
+                piece(order[2], 2)
+                last(0)
+                cross(z, 1)
+                last(1)
+                edge_in()
+        def between(i):
+            @pl.when(end)
+            def _():
+                piece(order[i + 1], 2)
+            if i == 0:
+                @pl.when(inside)
+                def _():
+                    piece(order[0], 2)
+
+        if more:
+            first_part(layer + 1, PARTS[0], x_s, between)
+
             @pl.when(inside)
             def _():
-                piece(order[0], 2)
-            ahead(1)
-            piece(order[1], 1)
-            ahead(2)
-            piece(order[1], 2)
-            last(3)
-            y_copy(z, 0).start()
-            ahead(3)
-            piece(order[2], 1)
-            piece(order[2], 2)
-            last(0)
-            for c in (1, 2):
-                cross(z, c)
-                last(c)
-            y_copy(z, 0).wait_recv()
-            own_part(z * 2, 0, EDGE)[...] += y_edge[...]
-            dest = x_s if layer + 1 < layers else out_ref
-            dest[...] = (a_ref[...].astype(F32) + own_part(z * 2)[...]).astype(BF16)
+                piece(order[1], 2)
+                piece(order[2], 2)
+            send_part(0)
+        with jax.named_scope('final'):
+            cross(z, 2)
+            last(2)
+            if more:
+                done(PARTS[1])
+            else:
+                done(WHOLE)
 
         for zz in range(NZ):
             for dy in range(2):
@@ -607,9 +734,11 @@
 
     start(attention_loads(0))
     start(cache_loads(0))
+    first_part(0, WHOLE, x_ref, lambda i: None)
+    for part in range(2):
+        send_part(part)
     for layer in range(layers):
-        attention(layer, x_ref if layer == 0 else x_s)
-        gather(layer)
+        gather(layer, x_ref if layer == 0 else x_s)
         all_experts(layer)
         if layer + 1 < layers:
             start(attention_loads(layer + 1))
@@ -641,8 +770,8 @@
                 buf((NZ * NY, TOK, D), F32), buf((NZ, TOK, D), F32), buf((EDGE, D), F32),
                 buf((NZ, TOK, D), F32), buf((NZ, EDGE, D), F32), buf((NZ, TOK, D), F32), buf((NZ, EDGE, D), F32),
                 sem((3, 4)), sem((21,)), sem((BLK,)), sem((BLK,)), sem((GROUP,)), sem((GROUP,)), sem((GROUP,)), sem((GROUP,)),
-                sem((NZ, 3, 2)), sem((NZ, 3)), sem((NZ, 2)), sem((NZ, 2)), sem((NZ, 2)), sem((NZ, 2)),
-                sem((NZ * NY,)), sem((NZ * NY,)), sem((NZ, 3)), sem((NZ, 3)), sem((NZ, 4)), sem((NZ, 4)), sem((NZ, 4)), sem((NZ, 4)),
+                sem((NZ, 3, 2)), sem((NZ, 3)), *[sem((NZ, 2))] * 4,
+                *[sem((NZ * NY,))] * 2, *[sem((NZ, 3))] * 2, *[sem((NZ, 4))] * 4,
             ],
             compiler_params=pltpu.CompilerParams(vmem_limit_bytes=67_043_328, collective_id=0, has_side_effects=True),
             name='layers',

time: 200 us -> 189 us (0.945)
  Pallas kernels: 198 us -> 187 us
    pallas_call x1, Pallas kernels: 198 us -> 187 us  [device_step(): pl.pallas_call(functools.partial(kernel, layers), out_shape=jax.ShapeDtyp...]
where the time goes in v4:
time: 189 us
  Pallas kernels  187 us (99%)
    pallas_call x1, Pallas kernels, device_step(): pl.pallas_call(functools.partial(kernel, layers), out_shape=jax.ShapeDtyp...  187 us

profile of v4, /device:TPU:0, one launch (start us, length us, event | category | flops | bytes accessed | tf_op | source)
XLA Modules:
  0.0 189.1 jit_solution(9873695335409573104)
XLA Ops:
  0.0 187.5 %layers.1 = bf16[128,896]{1,0:T(8,128)(2,1)} custom-call(bf16[128,896]{1,0:T(8,128)(2,1)} %x_ref.1, bf16[2,8,16,128,128]{4,3,2,1,0:T(8,128)(2,1)} %bitcast.4, bf16[2,8,16,128,128]{4,3,2,1,0:T(8,128)(2,1)} %bitcast.5, s32[1,128]{1,0:T(1,128)} %bitcast.7, bf16[2,896,2048]{2,1,0:T(8,128)(2,1)} %wq_hbm.1, bf16[2,896,512]{2,1,0:T(8,128)(2,1)} %wk_hbm.1, ...), custom_call_target="tpu_custom_call" | custom-call | tf_op jit(solution)/shard_map/layers/pallas_call | solution.py:758
  187.5 1.6 copy.15

commit v5 on v4

--- a/solution.py
+++ b/solution.py
@@ -486,7 +486,7 @@
             for i in range(LOCAL // chunk):
                 for copy in weights[3 * i:3 * i + 3]:
                     copy.wait()
-                lax.fori_loop(i * chunk, (i + 1) * chunk, functools.partial(experts, layer), 0)
+                lax.fori_loop(i * chunk, (i + 1) * chunk, functools.partial(experts, layer), 0, unroll=2)
 
     cut = list(HALVES)
 

time: 189 us -> 188 us (level)
  no operation moved by 1% of the time
where the time goes in v5:
time: 188 us
  Pallas kernels  186 us (99%)
    pallas_call x1, Pallas kernels, device_step(): pl.pallas_call(functools.partial(kernel, layers), out_shape=jax.ShapeDtyp...  186 us

profile of v5, /device:TPU:0, one launch (start us, length us, event | category | flops | bytes accessed | tf_op | source)
XLA Modules:
  0.0 187.9 jit_solution(12945680390003543892)
XLA Ops:
  0.0 186.3 %layers.1 = bf16[128,896]{1,0:T(8,128)(2,1)} custom-call(bf16[128,896]{1,0:T(8,128)(2,1)} %x_ref.1, bf16[2,8,16,128,128]{4,3,2,1,0:T(8,128)(2,1)} %bitcast.4, bf16[2,8,16,128,128]{4,3,2,1,0:T(8,128)(2,1)} %bitcast.5, s32[1,128]{1,0:T(1,128)} %bitcast.7, bf16[2,896,2048]{2,1,0:T(8,128)(2,1)} %wq_hbm.1, bf16[2,896,512]{2,1,0:T(8,128)(2,1)} %wk_hbm.1, ...), custom_call_target="tpu_custom_call" | custom-call | tf_op jit(solution)/shard_map/layers/pallas_call | solution.py:758
  186.3 1.6 copy.15
